TPU v7x, 32 devices: a whole 2x2x4 slice. The times are simulated.
32 devices in a mesh: row: 4 (over y, x), col: 8 (over z, core).
Axes of the slice: x: 2, y: 2, z: 4, core: 2. Of those that a mesh axis runs over, the one named last changes fastest.
Arguments:
- wrapped: float32 [1, 4096, 8192], P(None, 'row', 'col'), may hold values from -2.8 to 2.8
- col_steps: int32 [1, 4, 8], P(None, 'row', 'col'), may hold values from -2 to 2, as said below
- row_steps: int32 [1, 4, 8], P(None, 'row', 'col'), may hold values from -2 to 2, as said below
Outputs:
- unwrapped: float32 [1, 4096, 8192], P(None, 'row', 'col')
Inputs may be any that keep to these rules, and one draw needn't show every extreme that they name: `col_steps`: nonzero whole numbers; the last tile column has no edge. `row_steps`: nonzero whole numbers; the last tile row has no edge.
All inputs are finite; a program needn't handle non-finite values.
Results may differ from a plain program's by a relative error of at most 0.0003.
Values sent between devices are 32-bit elements; how exact they have to be, the bound alone decides.
A program may use at most 64 MiB of HBM per device.

v0:
```python
import functools
import math

import jax
import jax.numpy as jnp
from jax import lax
from jax.experimental import pallas as pl
from jax.experimental.pallas import tpu as pltpu
from jax.sharding import PartitionSpec as P

ITERS = 2
TWO_PI = 2.0 * math.pi
MESH = pl.DeviceIdType.MESH
LANES = 128
STRIP = 16


def cycles(change):
    return jnp.floor(change * (1.0 / TWO_PI) + 0.5)


def iota(shape, dim):
    return lax.broadcasted_iota(jnp.int32, shape, dim)


def total(values):
    return jnp.sum(values, axis=1, keepdims=True)


def shifted_in(values, first):
    lane = iota(values.shape, 1)
    return jnp.where(lane == 0, first, pltpu.roll(values, 1, 1))


def triangle(size, dim):
    ordered = iota((size, size), dim) <= iota((size, size), 1 - dim)
    return ordered.astype(jnp.float32).astype(jnp.bfloat16)


def line_counts(line, step):
    lane = iota(line.shape, 1)
    floors = jnp.where(lane == 0, 0.0, cycles(line - pltpu.roll(line, 1, 1)))
    floors = jnp.broadcast_to(floors, (16, line.shape[1]))
    upper, ones = triangle(step, 0), jnp.ones((step, step), jnp.bfloat16)
    earlier, counts = None, []
    for b in range(line.shape[1] // step):
        piece = floors[:, b * step : (b + 1) * step]
        count = jnp.dot(piece.astype(jnp.bfloat16), upper, preferred_element_type=jnp.float32)
        if b > 0:
            count = count + jnp.dot(
                earlier.astype(jnp.bfloat16), ones, preferred_element_type=jnp.float32
            )
        earlier = piece if b == 0 else earlier + piece
        counts.append(count[0:1, :])
    return jnp.concatenate(counts, axis=1)


def edge_kernel(
    names, sizes, rows_step, cols_step,
    wrapped, col_steps, row_steps,
    integ, offset,
    cells, left_out, up_out, right_in, below_in, corner_above, corner_left,
    last_row, end_lines, row_sums, floors, mine_out, every,
    load_sem, send_sem, recv_sem, gather_send, gather_recv, all_in,
):
    row_name, col_name = names
    grid_rows, grid_cols = sizes
    devices = grid_rows * grid_cols
    tile_rows, tile_cols = cells.shape
    my_row, my_col = lax.axis_index(row_name), lax.axis_index(col_name)
    me = my_row * grid_cols + my_col

    chunks = tile_rows // rows_step
    rest = pl.ds(LANES, tile_cols - LANES)
    regions = [(pl.ds(0, tile_rows), pl.ds(0, LANES)), (pl.ds(0, 16), rest)]
    for q in range(chunks):
        top = max(q * rows_step, 16)
        regions.append((pl.ds(top, (q + 1) * rows_step - top), rest))
    loads = []
    for k, (rows, cols) in enumerate(regions):
        loads.append(
            pltpu.make_async_copy(wrapped.at[0, rows, cols], cells.at[rows, cols], load_sem.at[k])
        )
        loads[-1].start()

    def row_place(p):
        return my_row, lax.rem(my_col + p, grid_cols)

    def col_place(p):
        return lax.rem(my_row + p, grid_rows), my_col

    def signal_all(semaphore, place, count):
        def signal(p, carry):
            pl.semaphore_signal(semaphore, inc=1, device_id=place(p), device_id_type=MESH)
            return carry

        lax.fori_loop(1, count, signal, 0)

    every[...] = jnp.zeros(every.shape, jnp.float32)

    barrier = pltpu.get_barrier_semaphore()
    signal_all(barrier, col_place, grid_rows)
    signal_all(barrier, row_place, grid_cols)

    with jax.named_scope("load_head"):
        loads[0].wait()
    with jax.named_scope("head"):
        for q in range(chunks):
            span = slice(q * rows_step, (q + 1) * rows_step)
            left_out[0:1, span] = cells[span, 0:LANES].T[0:1, :]
        left_out[1:2, :] = line_counts(left_out[0:1, :], rows_step)
    with jax.named_scope("load_top"):
        loads[1].wait()
    with jax.named_scope("first_row"):
        up_out[0:1, :] = cells[0:1, :]
        up_out[1:2, :] = line_counts(cells[0:1, :], cols_step)

    lane = iota((STRIP, LANES), 1)

    def strip(k, carry):
        rows = pl.ds(pl.multiple_of(k * STRIP, STRIP), STRIP)
        wrapped_around = cells[rows, 0:LANES]
        sums = jnp.zeros((STRIP, LANES), jnp.float32)
        for j in range(tile_cols // LANES):
            cols = slice(j * LANES, (j + 1) * LANES)
            here = cells[rows, cols]
            rolled = pltpu.roll(here, 1, 1)
            across = cycles(here - jnp.where(lane == 0, wrapped_around, rolled))
            wrapped_around = rolled
            floors[rows, cols] = across.astype(jnp.bfloat16)
            sums = sums + across
        row_sums[rows, :] = sums.astype(jnp.bfloat16)
        return carry

    per_chunk = rows_step // STRIP

    def set_floors(q):
        with jax.named_scope(f"floors_{q}"):
            lax.fori_loop(q * per_chunk, (q + 1) * per_chunk, strip, 0, unroll=math.gcd(per_chunk, 8))

    early = chunks // 2
    for q in range(early):
        loads[q + 2].wait()
        set_floors(q)

    with jax.named_scope("barrier"):
        pl.semaphore_wait(barrier, grid_rows + grid_cols - 2)
    corner = cells.at[pl.ds(tile_rows - 8, 8), pl.ds(tile_cols - LANES, LANES)]
    links = (
        (left_out, right_in, 0, -1, my_col > 0, my_col < grid_cols - 1),
        (up_out, below_in, -1, 0, my_row > 0, my_row < grid_rows - 1),
        (corner, corner_left, 0, 1, my_col < grid_cols - 1, my_col > 0),
        (corner, corner_above, 1, 0, my_row < grid_rows - 1, my_row > 0),
    )

    def link_copy(k, away):
        source, target, d_row, d_col, _, _ = links[k]
        place = (
            lax.rem(my_row + d_row * away + grid_rows, grid_rows),
            lax.rem(my_col + d_col * away + grid_cols, grid_cols),
        )
        return pltpu.make_async_remote_copy(
            src_ref=source, dst_ref=target, send_sem=send_sem.at[k], recv_sem=recv_sem.at[k],
            device_id=place, device_id_type=MESH,
        )

    def launch(k):
        sends, receives = links[k][4], links[k][5]

        @pl.when(sends)
        def _():
            link_copy(k, 1).start()

        @pl.when(jnp.logical_not(receives))
        def _():
            target = links[k][1]
            target[...] = jnp.zeros(target.shape, jnp.float32)

    launch(0)
    launch(1)
    signal_all(all_in, col_place, grid_rows)
    for q in range(early, chunks):
        loads[q + 2].wait()
    launch(3)
    launch(2)
    for q in range(early, chunks):
        set_floors(q)
    with jax.named_scope("ends"):
        ones = jnp.ones((16, LANES), jnp.bfloat16)
        for q in range(chunks):
            span = slice(q * rows_step, (q + 1) * rows_step)
            sums = lax.dot_general(
                ones, row_sums[span, :], (((1,), (1,)), ((), ())),
                preferred_element_type=jnp.float32,
            )
            end_lines[0:1, span] = left_out[1:2, span] + sums[0:1, :]
            end_lines[1:3, span] = cells[span, tile_cols - LANES :].T[LANES - 2 :, :]
    with jax.named_scope("last_row"):
        last_row[...] = left_out[1:2, tile_rows - 1 :] + line_counts(
            cells[tile_rows - 1 : tile_rows, :], cols_step
        )
    row_inner = cells[tile_rows - 2 : tile_rows - 1, :]
    row_outer = cells[tile_rows - 1 : tile_rows, :]

    with jax.named_scope("integrate"):
        upper, lower = triangle(cols_step, 0), triangle(rows_step, 1)
        down_carry = jnp.zeros((1, LANES), jnp.float32)
        for q in range(chunks):
            top = q * rows_step
            rows = pl.ds(top, rows_step)
            head = cells[rows, 0:LANES]
            above = cells[max(top - 1, 0) : max(top, 1), 0:LANES]
            before = jnp.where(iota(head.shape, 0) == 0, above, pltpu.roll(head, 1, 0))
            counts = down_carry + jnp.dot(
                lower, cycles(head - before).astype(jnp.bfloat16), preferred_element_type=jnp.float32
            )
            down_carry = counts[rows_step - 1 : rows_step, :]
            carry = counts[:, 0:1]
            for b in range(tile_cols // cols_step):
                cols = slice(b * cols_step, (b + 1) * cols_step)
                count = carry + jnp.dot(
                    floors[rows, cols], upper, preferred_element_type=jnp.float32
                )
                carry = count[:, cols_step - 1 : cols_step]
                integ[rows, cols] = cells[rows, cols] * (1.0 / TWO_PI) - count

    for k in range(4):

        with jax.named_scope(f"halo_{k}"):

            @pl.when(links[k][5])
            def _():
                link_copy(k, 1).wait_recv()

    def base(inner, outer, inner_before, outer_before, at_image_edge, first, count, beyond):
        over = cycles(outer - inner)
        over_before = shifted_in(over, cycles(outer_before - inner_before))
        along_outer = cycles(outer - shifted_in(outer, outer_before))
        along_inner = cycles(inner - shifted_in(inner, inner_before))
        charge = over_before + along_outer - over - along_inner
        charge = jnp.where((iota(charge.shape, 1) == 0) & at_image_edge, 0.0, charge)
        weight = 1.0 / (1.0 + jnp.abs(charge))
        jump = beyond - count - cycles(first - outer)
        return total(weight * jump) / total(weight)

    across_base = base(
        end_lines[1:2, :], end_lines[2:3, :],
        corner_above[7:8, LANES - 2 : LANES - 1], corner_above[7:8, LANES - 1 : LANES],
        my_row == 0, right_in[0:1, :], end_lines[0:1, :], right_in[1:2, :],
    ) + col_steps[0].astype(jnp.float32)
    down_base = base(
        row_inner, row_outer,
        corner_left[6:7, LANES - 1 : LANES], corner_left[7:8, LANES - 1 : LANES],
        my_col == 0, below_in[0:1, :], last_row[...], below_in[1:2, :],
    ) + row_steps[0].astype(jnp.float32)
    slot = iota((1, LANES), 1)
    mine_out[...] = jnp.where(
        slot == my_col, across_base, jnp.where(slot == grid_cols + my_col, down_base, 0.0)
    )

    def gather_copy(row, col, owner):
        peer = row * grid_cols + col
        return pltpu.make_async_remote_copy(
            src_ref=mine_out, dst_ref=every.at[owner], send_sem=gather_send.at[peer],
            recv_sem=gather_recv.at[owner], device_id=(row, col), device_id_type=MESH,
        )

    def span(low, high, act):
        def step(k, carry):
            act(k)
            return carry

        lax.fori_loop(low, high, step, 0)

    def each_target(act):
        first_row = jnp.where(my_row == 0, 1, jnp.where(my_col == 0, my_row + 1, grid_rows))
        span(first_row, grid_rows, lambda r: span(my_col + 1, grid_cols, lambda c: act(r, c)))
        span(my_col + 1, grid_cols, lambda c: act(my_row, c))
        span(my_row + 1, grid_rows, lambda r: act(r, my_col))

    def each_source(act):
        span(0, my_col, lambda c: act(my_row, c))
        span(0, my_row, lambda r: act(r, my_col))
        span(0, jnp.where(my_row > 0, my_col, 0), lambda c: act(0, c))
        span(1, jnp.where(my_col > 0, my_row, 0), lambda r: act(r, 0))

    with jax.named_scope("all_in"):
        pl.semaphore_wait(all_in, grid_rows - 1)
    with jax.named_scope("tell"):
        each_target(lambda r, c: gather_copy(r, c, me).start())
    with jax.named_scope("sent"):
        for k in range(4):

            @pl.when(links[k][4])
            def _():
                link_copy(k, 1).wait_send()

    with jax.named_scope("hear"):
        each_source(lambda r, c: gather_copy(r, c, r * grid_cols + c).wait_recv())

    padded = -(-grid_rows // 8) * 8
    tile_row = iota((padded, LANES), 0)
    tile_lane = iota((padded, LANES), 1)
    grid = jnp.zeros((padded, LANES), jnp.float32)
    for r in range(grid_rows):
        line = every[r * grid_cols]
        for c in range(1, grid_cols):
            line = line + every[r * grid_cols + c]
        grid = jnp.where(tile_row == r, line, grid)
    def summed(mask):
        picked = jnp.where(mask, grid, 0.0)
        return jnp.sum(jnp.sum(picked, axis=0, keepdims=True), axis=1, keepdims=True)

    earlier_cols = tile_lane < my_col
    across_here = summed((tile_row == my_row) & earlier_cols)
    across_top = summed((tile_row == 0) & earlier_cols)
    down_here = summed((tile_row < my_row) & (tile_lane == grid_cols + my_col))
    down_left = summed((tile_row < my_row) & (tile_lane == grid_cols))
    here = left = top = origin = jnp.zeros((1, 1), jnp.float32)
    for sweep in range(ITERS):
        prefix_across = across_here + (left - here)
        prefix_across_top = across_top + (origin - top)
        prefix_down = down_here + (top - here)
        prefix_down_left = down_left + (origin - left)
        here = here + 0.5 * (prefix_across + prefix_across_top + prefix_down + prefix_down_left)
        left = left + prefix_down_left
        top = top + prefix_across_top
    offset[...] = jnp.broadcast_to(here, offset.shape)
    each_target(lambda r, c: gather_copy(r, c, me).wait_send())


def place_kernel(integ, offset, out, ready, sems):
    parts = sems.shape[0]
    step = integ.shape[0] // parts
    shift = offset[0:1, 0:1]
    copies = []
    for q in range(parts):
        rows = pl.ds(q * step, step)
        ready[rows, :] = integ[rows, :] + shift
        copy = pltpu.make_async_copy(ready.at[rows], out.at[rows], sems.at[q])
        copy.start()
        copies.append(copy)
    for copy in copies:
        copy.wait()


def on_device(names, sizes, wrapped, col_steps, row_steps):
    frames, tile_rows, tile_cols = wrapped.shape
    devices = sizes[0] * sizes[1]
    rows_step = math.gcd(tile_rows, 256)
    cols_step = math.gcd(tile_cols, 256)
    f32 = jnp.float32
    call = pl.pallas_call(
        functools.partial(edge_kernel, names, sizes, rows_step, cols_step),
        out_shape=(
            pltpu.VMEM((tile_rows, tile_cols), f32),
            pltpu.VMEM((8, LANES), f32),
        ),
        in_specs=[
            pl.BlockSpec(memory_space=pltpu.HBM),
            pl.BlockSpec(memory_space=pltpu.VMEM),
            pl.BlockSpec(memory_space=pltpu.VMEM),
        ],
        out_specs=(
            pl.BlockSpec(memory_space=pltpu.VMEM),
            pl.BlockSpec(memory_space=pltpu.VMEM),
        ),
        scratch_shapes=[
            pltpu.VMEM((tile_rows, tile_cols), f32),
            pltpu.VMEM((2, tile_rows), f32),
            pltpu.VMEM((2, tile_cols), f32),
            pltpu.VMEM((2, tile_rows), f32),
            pltpu.VMEM((2, tile_cols), f32),
            pltpu.VMEM((8, LANES), f32),
            pltpu.VMEM((8, LANES), f32),
            pltpu.VMEM((1, tile_cols), f32),
            pltpu.VMEM((3, tile_rows), f32),
            pltpu.VMEM((tile_rows, LANES), jnp.bfloat16),
            pltpu.VMEM((tile_rows, tile_cols), jnp.bfloat16),
            pltpu.VMEM((1, LANES), f32),
            pltpu.VMEM((devices, 1, LANES), f32),
            pltpu.SemaphoreType.DMA((tile_rows // rows_step + 2,)),
            pltpu.SemaphoreType.DMA((4,)),
            pltpu.SemaphoreType.DMA((4,)),
            pltpu.SemaphoreType.DMA((devices,)),
            pltpu.SemaphoreType.DMA((devices,)),
            pltpu.SemaphoreType.REGULAR,
        ],
        compiler_params=pltpu.CompilerParams(
            collective_id=0, has_side_effects=True, vmem_limit_bytes=57 * 1024 * 1024
        ),
    )
    parts = math.gcd(tile_rows // 8, 16)
    place = pl.pallas_call(
        place_kernel,
        out_shape=jax.ShapeDtypeStruct((tile_rows, tile_cols), f32),
        in_specs=[pl.BlockSpec(memory_space=pltpu.VMEM), pl.BlockSpec(memory_space=pltpu.VMEM)],
        out_specs=pl.BlockSpec(memory_space=pltpu.HBM),
        scratch_shapes=[
            pltpu.VMEM((tile_rows, tile_cols), f32),
            pltpu.SemaphoreType.DMA((parts,)),
        ],
        compiler_params=pltpu.CompilerParams(vmem_limit_bytes=24 * 1024 * 1024),
    )
    outs = [
        place(*call(wrapped[f : f + 1], col_steps[f : f + 1], row_steps[f : f + 1]))
        for f in range(frames)
    ]
    return jnp.stack(outs)


def solution(mesh):
    spec = P(None, "row", "col")
    sizes = (mesh.shape["row"], mesh.shape["col"])
    return jax.shard_map(
        functools.partial(on_device, ("row", "col"), sizes),
        mesh=mesh, in_specs=(spec, spec, spec), out_specs=spec, check_vma=False,
    )
```

profile of v0, /device:TPU:4, one launch (start us, length us, event | category | flops | bytes accessed | tf_op | source)
XLA Modules:
  0.0 14.6 jit_solution(13963015673190875997)
XLA Ops:
  1.3 11.1 %shard_map.37 = (f32[1024,1024]{1,0:T(8,128)S(1)}, f32[8,128]{1,0:T(8,128)S(1)}) custom-call(f32[1,1024,1024]{2,1,0:T(8,128)} %wrapped.1, s32[1,1,1]{2,1,0:T(1,128)S(6)} %copy.4.col_steps, s32[1,1,1]{2,1,0:T(1,128)S(6)} %copy.5.row_steps), custom_call_target="tpu_custom_call" | custom-call | tf_op jit(solution)/shard_map/pallas_call | solution.py:406
  12.4 2.2 %shard_map.38 = f32[1024,1024]{1,0:T(8,128)} custom-call(f32[1024,1024]{1,0:T(8,128)S(1)} %get-tuple-element.7.integ, f32[8,128]{1,0:T(8,128)S(1)} %get-tuple-element.8.offset), custom_call_target="tpu_custom_call" | custom-call | tf_op jit(solution)/shard_map/pallas_call | solution.py:406
where the time goes:
time: 14.8 us; the launch traced here: 14.6 us
  Pallas kernels  13.3 us (90%)
  between operations  1.3 us (9%)
    pallas_call x1, Pallas kernels, on_device(): call(wrapped[f:f + 1], col_steps[f:f + 1], row_steps[f:f + 1])  11.1 us
    pallas_call x1, Pallas kernels, on_device(): place(*call(wrapped[f:f + 1], col_steps[f:f + 1], row_steps[f:f + 1]))  2.19 us

commit v1 on v0

v1 whole, which is shorter than its diff:
```python
import functools
import math

import jax
import jax.numpy as jnp
from jax import lax
from jax.experimental import pallas as pl
from jax.experimental.pallas import tpu as pltpu
from jax.sharding import PartitionSpec as P

ITERS = 2
TWO_PI = 2.0 * math.pi
MESH = pl.DeviceIdType.MESH
LANES = 128
STRIP = 16


def cycles(change):
    return jnp.floor(change * (1.0 / TWO_PI) + 0.5)


def iota(shape, dim):
    return lax.broadcasted_iota(jnp.int32, shape, dim)


def total(values):
    return jnp.sum(values, axis=1, keepdims=True)


def shifted_in(values, first):
    lane = iota(values.shape, 1)
    return jnp.where(lane == 0, first, pltpu.roll(values, 1, 1))


def triangle(size, dim):
    ordered = iota((size, size), dim) <= iota((size, size), 1 - dim)
    return ordered.astype(jnp.float32).astype(jnp.bfloat16)


def line_counts(line, step):
    lane = iota(line.shape, 1)
    floors = jnp.where(lane == 0, 0.0, cycles(line - pltpu.roll(line, 1, 1)))
    floors = jnp.broadcast_to(floors, (16, line.shape[1]))
    upper, ones = triangle(step, 0), jnp.ones((step, step), jnp.bfloat16)
    earlier, counts = None, []
    for b in range(line.shape[1] // step):
        piece = floors[:, b * step : (b + 1) * step]
        count = jnp.dot(piece.astype(jnp.bfloat16), upper, preferred_element_type=jnp.float32)
        if b > 0:
            count = count + jnp.dot(
                earlier.astype(jnp.bfloat16), ones, preferred_element_type=jnp.float32
            )
        earlier = piece if b == 0 else earlier + piece
        counts.append(count[0:1, :])
    return jnp.concatenate(counts, axis=1)


def edge_kernel(
    names, sizes, rows_step, cols_step,
    wrapped, col_steps, row_steps,
    integ, offset,
    cells, left_out, right_in, rows_out, rows_in, corner_above, corner_diag,
    first_counts, end_lines, row_sums, floors, steps_across, steps_down, mine_h, mine_u,
    row_h, top_h, col_u, left_u,
    recv_sem, row_recv, top_recv, col_recv, left_recv, diag_in, row_in, far_in,
    load_sem, send_sem, h_send, u_send,
):
    row_name, col_name = names
    grid_rows, grid_cols = sizes
    tile_rows, tile_cols = cells.shape
    my_row, my_col = lax.axis_index(row_name), lax.axis_index(col_name)

    chunks = tile_rows // rows_step
    rest = pl.ds(LANES, tile_cols - LANES)
    regions = [
        (pl.ds(0, tile_rows), pl.ds(0, LANES)),
        (pl.ds(tile_rows - 16, 16), rest),
        (pl.ds(0, 16), rest),
    ]
    for q in range(chunks):
        top = max(q * rows_step, 16)
        bottom = min((q + 1) * rows_step, tile_rows - 16)
        regions.append((pl.ds(top, bottom - top), rest))
    loads = []
    for k, (rows, cols) in enumerate(regions):
        loads.append(
            pltpu.make_async_copy(wrapped.at[0, rows, cols], cells.at[rows, cols], load_sem.at[k])
        )
        loads[-1].start()
    for source, target in ((col_steps, steps_across), (row_steps, steps_down)):
        loads.append(pltpu.make_async_copy(source, target, load_sem.at[len(loads)]))
        loads[-1].start()

    def span(low, high, act):
        def step(k, carry):
            act(k)
            return carry

        lax.fori_loop(low, high, step, 0)

    def rows_below(act):
        span(my_row + 1, grid_rows, lambda r: act(r, my_col))

    def cols_right(act):
        span(my_col + 1, grid_cols, lambda c: act(my_row, c))

    def far_from_top(act):
        first = jnp.where(my_row == 0, 1, grid_rows)
        span(first, grid_rows, lambda r: span(my_col + 1, grid_cols, lambda c: act(r, c)))

    def far_from_left(act):
        first = jnp.where((my_row > 0) & (my_col == 0), my_row + 1, grid_rows)
        span(first, grid_rows, lambda r: span(1, grid_cols, lambda c: act(r, c)))

    def rows_further_below(act):
        span(my_row + 2, grid_rows, lambda r: act(r, my_col))

    def rows_further_above(act):
        span(0, my_row - 1, lambda r: act(r, my_col))

    def cols_left(act):
        span(0, my_col, lambda c: act(my_row, c))

    def tops_left(act):
        span(0, jnp.where(my_row > 0, my_col, 0), lambda c: act(0, c))

    def lefts_above(act):
        span(1, jnp.where(my_col > 0, my_row, 0), lambda r: act(r, 0))

    has_left, has_right = my_col > 0, my_col < grid_cols - 1
    has_above, has_below = my_row > 0, my_row < grid_rows - 1
    inner_diag = (my_row > 0) & (my_col > 0) & has_right & has_below
    inner_back = (my_row > 1) & (my_col > 1)

    zero_line = jnp.zeros((1, LANES), jnp.float32)
    for slots in (row_h, top_h, col_u, left_u):
        for k in range(slots.shape[0]):
            slots[k] = zero_line

    barrier = pltpu.get_barrier_semaphore()

    def await_signals(semaphore, count):

        @pl.when(count > 0)
        def _():
            pl.semaphore_wait(semaphore, count)

    def greet(semaphore):
        return lambda r, c: pl.semaphore_signal(
            semaphore, inc=1, device_id=(r, c), device_id_type=MESH
        )

    cols_right(greet(barrier))
    rows_further_below(greet(barrier))
    far_from_top(greet(barrier))
    far_from_left(greet(barrier))

    @pl.when(inner_diag)
    def _():
        greet(barrier)(my_row + 1, my_col + 1)

    @pl.when(has_above)
    def _():
        greet(barrier)(my_row - 1, my_col)

    @pl.when(jnp.logical_not(has_right))
    def _():
        right_in[...] = jnp.zeros(right_in.shape, jnp.float32)

    @pl.when(jnp.logical_not(has_above))
    def _():
        corner_above[...] = jnp.zeros(corner_above.shape, jnp.float32)

    @pl.when(jnp.logical_not(has_above & has_left))
    def _():
        corner_diag[...] = jnp.zeros(corner_diag.shape, jnp.float32)

    corner = cells.at[pl.ds(tile_rows - 8, 8), pl.ds(tile_cols - LANES, LANES)]
    links = (
        (left_out, right_in, 0, -1, has_left, has_right),
        (corner, corner_above, 1, 0, has_below, has_above),
        (rows_out, rows_in, 1, 0, has_below, has_above),
        (corner, corner_diag, 1, 1, has_below & has_right, has_above & has_left),
    )

    def link_copy(k):
        source, target, d_row, d_col, _, _ = links[k]
        place = (
            lax.rem(my_row + d_row + grid_rows, grid_rows),
            lax.rem(my_col + d_col + grid_cols, grid_cols),
        )
        return pltpu.make_async_remote_copy(
            src_ref=source, dst_ref=target, send_sem=send_sem.at[k], recv_sem=recv_sem.at[k],
            device_id=place, device_id_type=MESH,
        )

    first = my_row == grid_rows - 1
    last = (my_row == 0) & (my_col <= 1)
    between = jnp.logical_not(first | last)

    def enter():
        sources = my_col + jnp.maximum(my_row - 1, 0)
        sources = sources + jnp.where(my_row > 0, my_col, 0)
        sources = sources + jnp.where((my_col > 0) & (my_row > 0), my_row - 1, 0)
        sources = sources + jnp.where(inner_back, 1, 0) + jnp.where(has_below, 1, 0)
        await_signals(barrier, sources)

        cols_left(greet(row_in))
        rows_further_above(greet(far_in))
        tops_left(greet(far_in))
        lefts_above(greet(far_in))

        @pl.when(has_above & has_left)
        def _():
            greet(diag_in)(my_row - 1, my_col - 1)

    def push_left():

        @pl.when(has_left)
        def _():
            link_copy(0).start()

    def push_down():

        @pl.when(has_below)
        def _():
            link_copy(1).start()
            link_copy(2).start()

    with jax.named_scope("enter_0"):
        pl.when(first)(enter)

    with jax.named_scope("load_head"):
        loads[0].wait()
    with jax.named_scope("head"):
        for q in range(chunks):
            part = slice(q * rows_step, (q + 1) * rows_step)
            left_out[0:1, part] = cells[part, 0:LANES].T[0:1, :]
        left_out[1:2, :] = line_counts(left_out[0:1, :], rows_step)

    with jax.named_scope("enter_1"):
        pl.when(between)(enter)
        pl.when(jnp.logical_not(last))(push_left)

    with jax.named_scope("load_edges"):
        loads[1].wait()
        loads[-1].wait()
        loads[-2].wait()
    with jax.named_scope("last_row"):
        down_steps = steps_down[0].astype(jnp.float32)
        rows_out[0:1, :] = cells[tile_rows - 1 : tile_rows, :]
        rows_out[1:2, :] = cells[tile_rows - 2 : tile_rows - 1, :]
        rows_out[2:3, :] = (left_out[1:2, tile_rows - 1 :] - down_steps) + line_counts(
            cells[tile_rows - 1 : tile_rows, :], cols_step
        )

    pl.when(jnp.logical_not(last))(push_down)

    lane = iota((STRIP, LANES), 1)

    def strip(k, carry):
        rows = pl.ds(pl.multiple_of(k * STRIP, STRIP), STRIP)
        wrapped_around = cells[rows, 0:LANES]
        sums = jnp.zeros((STRIP, LANES), jnp.float32)
        for j in range(tile_cols // LANES):
            cols = slice(j * LANES, (j + 1) * LANES)
            here = cells[rows, cols]
            rolled = pltpu.roll(here, 1, 1)
            across = cycles(here - jnp.where(lane == 0, wrapped_around, rolled))
            wrapped_around = rolled
            floors[rows, cols] = across.astype(jnp.bfloat16)
            sums = sums + across
        row_sums[rows, :] = sums.astype(jnp.bfloat16)
        return carry

    per_chunk = rows_step // STRIP
    ones = jnp.ones((16, LANES), jnp.bfloat16)
    loads[2].wait()
    for q in range(chunks):
        with jax.named_scope(f"load_{q}"):
            loads[q + 3].wait()
        with jax.named_scope(f"floors_{q}"):
            lax.fori_loop(
                q * per_chunk, (q + 1) * per_chunk, strip, 0, unroll=math.gcd(per_chunk, 8)
            )
        if q == (chunks - 1) // 2:
            with jax.named_scope("enter_2"):

                @pl.when(last)
                def _():
                    enter()
                    push_left()
                    push_down()

    with jax.named_scope("ends"):
        for q in range(chunks):
            part = slice(q * rows_step, (q + 1) * rows_step)
            sums = lax.dot_general(
                ones, row_sums[part, :], (((1,), (1,)), ((), ())),
                preferred_element_type=jnp.float32,
            )
            end_lines[0:1, part] = left_out[1:2, part] + sums[0:1, :]
            end_lines[1:3, part] = cells[part, tile_cols - LANES :].T[LANES - 2 :, :]

    def arrived(k):

        @pl.when(links[k][5])
        def _():
            link_copy(k).wait_recv()

    def base(inner, outer, inner_before, outer_before, at_image_edge, first, count, beyond):
        over = cycles(outer - inner)
        over_before = shifted_in(over, cycles(outer_before - inner_before))
        along_outer = cycles(outer - shifted_in(outer, outer_before))
        along_inner = cycles(inner - shifted_in(inner, inner_before))
        charge = over_before + along_outer - over - along_inner
        charge = jnp.where((iota(charge.shape, 1) == 0) & at_image_edge, 0.0, charge)
        weight = 1.0 / (1.0 + jnp.abs(charge))
        jump = beyond - count - cycles(first - outer)
        return total(weight * jump) / total(weight)

    with jax.named_scope("halo_0"):
        arrived(0)
    with jax.named_scope("halo_1"):
        arrived(1)
    with jax.named_scope("base_h"):
        across_base = base(
            end_lines[1:2, :], end_lines[2:3, :],
            corner_above[7:8, LANES - 2 : LANES - 1], corner_above[7:8, LANES - 1 : LANES],
            my_row == 0, right_in[0:1, :], end_lines[0:1, :], right_in[1:2, :],
        ) + steps_across[0].astype(jnp.float32)
        mine_h[...] = jnp.broadcast_to(across_base, mine_h.shape)

    def h_copy(row, col, target, semaphore, owner):
        return pltpu.make_async_remote_copy(
            src_ref=mine_h, dst_ref=target.at[owner], send_sem=h_send.at[row * grid_cols + col],
            recv_sem=semaphore, device_id=(row, col), device_id_type=MESH,
        )

    def u_copy(row, col, target, semaphore, owner):
        return pltpu.make_async_remote_copy(
            src_ref=mine_u, dst_ref=target.at[owner], send_sem=u_send.at[row * grid_cols + col],
            recv_sem=semaphore, device_id=(row, col), device_id_type=MESH,
        )

    def row_copy(r, c, owner):
        return h_copy(r, c, row_h, row_recv, owner)

    def top_copy(r, c, owner):
        return h_copy(r, c, top_h, top_recv, owner)

    def col_copy(r, c, owner):
        return u_copy(r, c, col_u, col_recv, owner)

    def left_copy(r, c, owner):
        return u_copy(r, c, left_u, left_recv, owner)

    with jax.named_scope("row_in"):
        await_signals(row_in, grid_cols - 1 - my_col)
    with jax.named_scope("tell_row"):
        cols_right(lambda r, c: row_copy(r, c, my_col).start())

    with jax.named_scope("diag_in"):

        @pl.when(has_below & has_right)
        def _():
            pl.semaphore_wait(diag_in, 1)
            link_copy(3).start()

    with jax.named_scope("first_row"):

        @pl.when(has_above)
        def _():
            first_counts[...] = line_counts(cells[0:1, :], cols_step)

    with jax.named_scope("halo_2"):
        arrived(2)
        arrived(3)
    with jax.named_scope("base_u"):

        @pl.when(has_above)
        def _():
            down_base = base(
                rows_in[1:2, :], rows_in[0:1, :],
                corner_diag[6:7, LANES - 1 : LANES], corner_diag[7:8, LANES - 1 : LANES],
                my_col == 0, cells[0:1, :], rows_in[2:3, :], first_counts[...],
            )
            mine_u[...] = jnp.broadcast_to(down_base, mine_u.shape)

        @pl.when(jnp.logical_not(has_above))
        def _():
            mine_u[...] = zero_line

    with jax.named_scope("far_in"):
        below = grid_rows - 1 - my_row
        right = grid_cols - 1 - my_col
        edge = jnp.where((my_row == 0) | (my_col == 0), right, 0)
        await_signals(far_in, jnp.maximum(below - 1, 0) + below * edge)

    to_left_u = jnp.where((my_row > 0) & (my_col == 0), my_row, grid_rows)

    def all_left_u(act):
        span(to_left_u, grid_rows, lambda r: span(1, grid_cols, lambda c: act(r, c)))

    def rows_below_u(act):
        span(jnp.where(my_row > 0, my_row + 1, grid_rows), grid_rows, lambda r: act(r, my_col))

    with jax.named_scope("tell_far"):
        far_from_top(lambda r, c: top_copy(r, c, my_col).start())
        rows_below_u(lambda r, c: col_copy(r, c, my_row).start())
        all_left_u(lambda r, c: left_copy(r, c, my_row).start())

    with jax.named_scope("integrate"):
        upper, lower = triangle(cols_step, 0), triangle(rows_step, 1)
        down_carry = jnp.zeros((1, LANES), jnp.float32)
        for q in range(chunks):
            top = q * rows_step
            rows = pl.ds(top, rows_step)
            head = cells[rows, 0:LANES]
            above = cells[max(top - 1, 0) : max(top, 1), 0:LANES]
            before = jnp.where(iota(head.shape, 0) == 0, above, pltpu.roll(head, 1, 0))
            counts = down_carry + jnp.dot(
                lower, cycles(head - before).astype(jnp.bfloat16), preferred_element_type=jnp.float32
            )
            down_carry = counts[rows_step - 1 : rows_step, :]
            carry = counts[:, 0:1]
            for b in range(tile_cols // cols_step):
                cols = slice(b * cols_step, (b + 1) * cols_step)
                count = carry + jnp.dot(
                    floors[rows, cols], upper, preferred_element_type=jnp.float32
                )
                carry = count[:, cols_step - 1 : cols_step]
                integ[rows, cols] = cells[rows, cols] * (1.0 / TWO_PI) - count

    with jax.named_scope("sent"):
        for k in range(4):

            @pl.when(links[k][4])
            def _():
                link_copy(k).wait_send()

        cols_right(lambda r, c: row_copy(r, c, my_col).wait_send())
        far_from_top(lambda r, c: top_copy(r, c, my_col).wait_send())
        rows_below_u(lambda r, c: col_copy(r, c, my_row).wait_send())
        all_left_u(lambda r, c: left_copy(r, c, my_row).wait_send())

    def hear(slots, semaphore, first, count):
        for n in range(1, slots.shape[0]):

            @pl.when(count == n)
            def _():
                landed = slots.at[pl.ds(first, n)]
                pltpu.make_async_copy(landed, landed, semaphore).wait()

    with jax.named_scope("hear"):
        hear(row_h, row_recv, 0, my_col)
        hear(top_h, top_recv, 0, jnp.where(has_above, my_col, 0))
        hear(col_u, col_recv, 1, jnp.maximum(my_row - 1, 0))
        hear(left_u, left_recv, 1, jnp.where(has_left, my_row, 0))

    with jax.named_scope("finish"):

        def summed(slots):
            line = slots[0]
            for k in range(1, slots.shape[0]):
                line = line + slots[k]
            return line

        across_here = summed(row_h)
        across_top = jnp.where(has_above, summed(top_h), across_here)
        down_here = summed(col_u) + mine_u[...]
        down_left = jnp.where(has_left, summed(left_u), down_here)
        here = left = top = origin = zero_line
        for sweep in range(ITERS):
            prefix_across = across_here + (left - here)
            prefix_across_top = across_top + (origin - top)
            prefix_down = down_here + (top - here)
            prefix_down_left = down_left + (origin - left)
            here = here + 0.5 * (prefix_across + prefix_across_top + prefix_down + prefix_down_left)
            left = left + prefix_down_left
            top = top + prefix_across_top
        offset[...] = jnp.broadcast_to(here, offset.shape)


def place_kernel(integ, offset, out, ready, sems):
    parts = sems.shape[0]
    step = integ.shape[0] // parts
    shift = offset[0:1, 0:1]
    copies = []
    for q in range(parts):
        rows = pl.ds(q * step, step)
        ready[rows, :] = integ[rows, :] + shift
        copy = pltpu.make_async_copy(ready.at[rows], out.at[rows], sems.at[q])
        copy.start()
        copies.append(copy)
    for copy in copies:
        copy.wait()


def on_device(names, sizes, wrapped, col_steps, row_steps):
    frames, tile_rows, tile_cols = wrapped.shape
    devices = sizes[0] * sizes[1]
    rows_step = math.gcd(tile_rows, 256)
    cols_step = math.gcd(tile_cols, 256)
    f32 = jnp.float32


    def with_local_semaphores(*refs):
        dma = pltpu.SemaphoreType.DMA
        pl.run_scoped(
            functools.partial(edge_kernel, names, sizes, rows_step, cols_step, *refs),
            dma((tile_rows // rows_step + 5,)), dma((4,)), dma((devices,)), dma((devices,)),
        )

    call = pl.pallas_call(
        with_local_semaphores,
        out_shape=(
            pltpu.VMEM((tile_rows, tile_cols), f32),
            pltpu.VMEM((8, LANES), f32),
        ),
        in_specs=[
            pl.BlockSpec(memory_space=pltpu.HBM),
            pl.BlockSpec(memory_space=pltpu.HBM),
            pl.BlockSpec(memory_space=pltpu.HBM),
        ],
        out_specs=(
            pl.BlockSpec(memory_space=pltpu.VMEM),
            pl.BlockSpec(memory_space=pltpu.VMEM),
        ),
        scratch_shapes=[
            pltpu.VMEM((tile_rows, tile_cols), f32),
            pltpu.VMEM((2, tile_rows), f32),
            pltpu.VMEM((2, tile_rows), f32),
            pltpu.VMEM((3, tile_cols), f32),
            pltpu.VMEM((3, tile_cols), f32),
            pltpu.VMEM((8, LANES), f32),
            pltpu.VMEM((8, LANES), f32),
            pltpu.VMEM((1, tile_cols), f32),
            pltpu.VMEM((3, tile_rows), f32),
            pltpu.VMEM((tile_rows, LANES), jnp.bfloat16),
            pltpu.VMEM((tile_rows, tile_cols), jnp.bfloat16),
            pltpu.VMEM((1, 1, 1), jnp.int32),
            pltpu.VMEM((1, 1, 1), jnp.int32),
            pltpu.VMEM((1, LANES), f32),
            pltpu.VMEM((1, LANES), f32),
            pltpu.VMEM((sizes[1], 1, LANES), f32),
            pltpu.VMEM((sizes[1], 1, LANES), f32),
            pltpu.VMEM((sizes[0], 1, LANES), f32),
            pltpu.VMEM((sizes[0], 1, LANES), f32),
            pltpu.SemaphoreType.DMA((4,)),
            pltpu.SemaphoreType.DMA,
            pltpu.SemaphoreType.DMA,
            pltpu.SemaphoreType.DMA,
            pltpu.SemaphoreType.DMA,
            pltpu.SemaphoreType.REGULAR,
            pltpu.SemaphoreType.REGULAR,
            pltpu.SemaphoreType.REGULAR,
        ],
        compiler_params=pltpu.CompilerParams(
            collective_id=0, has_side_effects=True, vmem_limit_bytes=57 * 1024 * 1024
        ),
    )
    parts = math.gcd(tile_rows // 8, 16)
    place = pl.pallas_call(
        place_kernel,
        out_shape=jax.ShapeDtypeStruct((tile_rows, tile_cols), f32),
        in_specs=[pl.BlockSpec(memory_space=pltpu.VMEM), pl.BlockSpec(memory_space=pltpu.VMEM)],
        out_specs=pl.BlockSpec(memory_space=pltpu.HBM),
        scratch_shapes=[
            pltpu.VMEM((tile_rows, tile_cols), f32),
            pltpu.SemaphoreType.DMA((parts,)),
        ],
        compiler_params=pltpu.CompilerParams(vmem_limit_bytes=24 * 1024 * 1024),
    )
    outs = [
        place(*call(wrapped[f : f + 1], col_steps[f : f + 1], row_steps[f : f + 1]))
        for f in range(frames)
    ]
    return jnp.stack(outs)


def solution(mesh):
    spec = P(None, "row", "col")
    sizes = (mesh.shape["row"], mesh.shape["col"])
    return jax.shard_map(
        functools.partial(on_device, ("row", "col"), sizes),
        mesh=mesh, in_specs=(spec, spec, spec), out_specs=spec, check_vma=False,
    )
```

time: 14.8 us -> 13.6 us (0.919)
  the two profiles are of different devices: /device:TPU:4 before, /device:TPU:12 now
where the time goes in v1:
time: 13.6 us; the launch traced here: 13.4 us
  Pallas kernels  12.1 us (89%)
  between operations  1.3 us (10%)
    pallas_call x1, Pallas kernels, on_device(): call(wrapped[f:f + 1], col_steps[f:f + 1], row_steps[f:f + 1])  9.94 us
    pallas_call x1, Pallas kernels, on_device(): place(*call(wrapped[f:f + 1], col_steps[f:f + 1], row_steps[f:f + 1]))  2.19 us

profile of v1, /device:TPU:12, one launch (start us, length us, event | category | flops | bytes accessed | tf_op | source)
XLA Modules:
  0.0 13.4 jit_solution(5072612562271142073)
XLA Ops:
  1.3 9.9 %shard_map.37 = (f32[1024,1024]{1,0:T(8,128)S(1)}, f32[8,128]{1,0:T(8,128)S(1)}) custom-call(f32[1,1024,1024]{2,1,0:T(8,128)} %refs_0_.1, s32[1,1,1]{2,1,0:T(1,128)S(6)} %copy.4.refs_1_, s32[1,1,1]{2,1,0:T(1,128)S(6)} %copy.5.refs_2_), custom_call_target="tpu_custom_call" | custom-call | tf_op jit(solution)/shard_map/pallas_call | solution.py:576
  11.2 2.2 %shard_map.38 = f32[1024,1024]{1,0:T(8,128)} custom-call(f32[1024,1024]{1,0:T(8,128)S(1)} %get-tuple-element.7.integ, f32[8,128]{1,0:T(8,128)S(1)} %get-tuple-element.8.offset), custom_call_target="tpu_custom_call" | custom-call | tf_op jit(solution)/shard_map/pallas_call | solution.py:576

commit v2 on v1

v2 whole, which is shorter than its diff:
```python
import functools
import math

import jax
import jax.numpy as jnp
from jax import lax
from jax.experimental import pallas as pl
from jax.experimental.pallas import tpu as pltpu
from jax.sharding import PartitionSpec as P

ITERS = 2
TWO_PI = 2.0 * math.pi
MESH = pl.DeviceIdType.MESH
LANES = 128
STRIP = 16
RELAYS = 2


def cycles(change):
    return jnp.floor(change * (1.0 / TWO_PI) + 0.5)


def iota(shape, dim):
    return lax.broadcasted_iota(jnp.int32, shape, dim)


def total(values):
    return jnp.sum(values, axis=1, keepdims=True)


def previous(line, first):
    lane, row = iota(line.shape, 1), iota(line.shape, 0)
    along = pltpu.roll(line, 1, 1)
    across = pltpu.roll(along, 1, 0) if line.shape[0] > 1 else along
    return jnp.where(lane > 0, along, jnp.where(row > 0, across, first))


def summed(line):
    return total(jnp.sum(line, axis=0, keepdims=True))


def triangle(size, dim):
    ordered = iota((size, size), dim) <= iota((size, size), 1 - dim)
    return ordered.astype(jnp.float32).astype(jnp.bfloat16)


def line_counts(line):
    groups = line.shape[0]
    row = iota(line.shape, 0)
    floors = cycles(line - previous(line, line[0:1, 0:1]))
    whole, shift = floors, 1
    while shift < groups:
        whole = whole + jnp.where(row >= shift, pltpu.roll(whole, shift, 0), 0.0)
        shift *= 2
    pair = jnp.concatenate([floors, whole - floors], axis=1)
    pair = jnp.concatenate([pair] * (-(-16 // groups)), axis=0).astype(jnp.bfloat16)
    ones = jnp.ones((LANES, LANES), jnp.bfloat16)
    table = jnp.concatenate([triangle(LANES, 0), ones], axis=0)
    return jnp.dot(pair, table, preferred_element_type=jnp.float32)[0:groups, :]


def weights(inner, outer, inner_before, outer_before, at_image_edge):
    over = cycles(outer - inner)
    over_before = previous(over, cycles(outer_before - inner_before))
    along_outer = cycles(outer - previous(outer, outer_before))
    along_inner = cycles(inner - previous(inner, inner_before))
    charge = over_before + along_outer - over - along_inner
    start = (iota(charge.shape, 1) == 0) & (iota(charge.shape, 0) == 0)
    charge = jnp.where(start & at_image_edge, 0.0, charge)
    return 1.0 / (1.0 + jnp.abs(charge))


def mismatch(weight, outer, count, first, beyond):
    jump = beyond - count - cycles(first - outer)
    return summed(weight * jump) / summed(weight)


def edge_kernel(
    names, sizes, rows_step, cols_step,
    wrapped, col_steps, row_steps,
    integ, offset,
    cells, left_out, right_in, corner_above, corner_left, tops, bottom_out, bottoms, inner_row,
    floors, row_sums, steps_across, steps_down, mine_h, mine_y, row_h, top_h, col_h, left_d,
    link_recv, top_recv, bottom_recv, row_recv, far_recv, row_in, col_in, far_in,
    load_sem, link_send, top_send, bottom_send, h_send, c_send, t_send, d_send,
):
    row_name, col_name = names
    grid_rows, grid_cols = sizes
    tile_rows, tile_cols = cells.shape
    my_row, my_col = lax.axis_index(row_name), lax.axis_index(col_name)
    down, right = tile_rows // LANES, tile_cols // LANES

    chunks = tile_rows // rows_step
    rest = pl.ds(LANES, tile_cols - LANES)
    regions = [
        (pl.ds(0, tile_rows), pl.ds(0, LANES)),
        (pl.ds(tile_rows - 16, 16), rest),
        (pl.ds(0, 16), rest),
    ]
    for q in range(chunks):
        top = max(q * rows_step, 16)
        bottom = min((q + 1) * rows_step, tile_rows - 16)
        regions.append((pl.ds(top, bottom - top), rest))
    loads = []
    for k, (rows, cols) in enumerate(regions):
        loads.append(
            pltpu.make_async_copy(wrapped.at[0, rows, cols], cells.at[rows, cols], load_sem.at[k])
        )
        loads[-1].start()
    for source, target in ((col_steps, steps_across), (row_steps, steps_down)):
        loads.append(pltpu.make_async_copy(source, target, load_sem.at[len(loads)]))
        loads[-1].start()

    def span(low, high, act):
        def step(k, carry):
            act(k)
            return carry

        lax.fori_loop(low, high, step, 0)

    def along_row(low, high, act):
        span(low, high, lambda c: act(my_row, c))

    def along_col(low, high, act):
        span(low, high, lambda r: act(r, my_col))

    has_left, has_right = my_col > 0, my_col < grid_cols - 1
    has_above, has_below = my_row > 0, my_row < grid_rows - 1
    near = jnp.minimum(my_row + 3, grid_rows)
    relayed = my_col < RELAYS
    direct_top = (my_row == 0) & jnp.logical_not(relayed)

    def far_below(act):
        low = jnp.where(direct_top, 1, grid_rows)
        span(low, grid_rows, lambda r: span(my_col + 1, grid_cols, lambda c: act(r, c)))

    def direct_tops(act):
        span(RELAYS, jnp.where(has_above, my_col, 0), lambda c: act(0, c))

    zero_line = jnp.zeros((1, LANES), jnp.float32)
    for slots in (row_h, top_h):
        for k in range(grid_cols):
            slots[k] = zero_line

    barrier = pltpu.get_barrier_semaphore()

    def await_signals(semaphore, count):

        @pl.when(count > 0)
        def _():
            pl.semaphore_wait(semaphore, count)

    def greet(semaphore):
        return lambda r, c: pl.semaphore_signal(
            semaphore, inc=1, device_id=(r, c), device_id_type=MESH
        )

    along_row(my_col + 1, grid_cols, greet(barrier))
    along_row(jnp.where(has_below, jnp.maximum(my_col - 1, 0), my_col), my_col, greet(barrier))
    along_col(jnp.maximum(my_row - 2, 0), my_row, greet(barrier))
    along_col(my_row + 3, grid_rows, greet(barrier))
    far_below(greet(barrier))

    def clear(ref, unless):

        @pl.when(jnp.logical_not(unless))
        def _():
            ref[...] = jnp.zeros(ref.shape, ref.dtype)

    clear(right_in, has_right)
    clear(corner_above, has_above)
    clear(corner_left, has_left & has_below)
    clear(mine_y, has_above)

    first = jnp.logical_not(has_below)
    last = (my_row == 0) & relayed
    between = jnp.logical_not(first | last)

    def enter():
        sources = my_col + jnp.maximum(my_row - 2, 0)
        sources = sources + jnp.where(has_above, jnp.maximum(my_col - RELAYS, 0), 0)
        sources = sources + (near - 1 - my_row) + jnp.where(has_right & has_below, 1, 0)
        await_signals(barrier, sources)
        along_row(0, jnp.where(has_below, my_col - 1, my_col), greet(row_in))
        along_col(0, my_row - 2, greet(col_in))
        direct_tops(greet(far_in))

    corner = cells.at[pl.ds(tile_rows - 8, 8), pl.ds(tile_cols - LANES, LANES)]
    links = (
        (left_out, right_in, 0, -1, has_left, has_right),
        (corner, corner_above, 1, 0, has_below, has_above),
        (corner, corner_left, 0, 1, has_right & has_below, has_left & has_below),
    )

    def link_copy(k):
        source, target, d_row, d_col, _, _ = links[k]
        place = (
            lax.rem(my_row + d_row + grid_rows, grid_rows),
            lax.rem(my_col + d_col + grid_cols, grid_cols),
        )
        return pltpu.make_async_remote_copy(
            src_ref=source, dst_ref=target, send_sem=link_send.at[k], recv_sem=link_recv.at[k],
            device_id=place, device_id_type=MESH,
        )

    def push(k):

        @pl.when(links[k][4])
        def _():
            link_copy(k).start()

    def arrived(k):

        @pl.when(links[k][5])
        def _():
            link_copy(k).wait_recv()

    def send(source, target, send_sem, recv_sem, place):
        return pltpu.make_async_remote_copy(
            src_ref=source, dst_ref=target, send_sem=send_sem, recv_sem=recv_sem,
            device_id=place, device_id_type=MESH,
        )

    def top_copy(r, c):
        line = tops.at[my_row]
        return send(line, line, top_send.at[r], top_recv, (r, c))

    def bottom_copy(r, c):
        return send(bottom_out, bottoms.at[my_row], bottom_send.at[r], bottom_recv, (r, c))

    def row_copy(r, c):
        return send(mine_h, row_h.at[my_col], h_send.at[r * grid_cols + c], row_recv, (r, c))

    def far_copy(r, c):
        return send(mine_h, top_h.at[my_col], h_send.at[r * grid_cols + c], far_recv, (r, c))

    def relay_in(r, c):
        return send(mine_h, col_h, c_send.at[r], link_recv.at[3], (r, c))

    def relay_out(r, c):
        return send(col_h, top_h.at[my_col], t_send.at[c], far_recv, (r, c))

    def left_copy(r, c):
        return send(mine_y, left_d, d_send.at[c], link_recv.at[4], (r, c))

    def push_tops(low, high, act):
        along_col(jnp.where(has_above, low, grid_rows), high, act)

    def push_bottoms():
        along_col(my_row + 1, near, lambda r, c: bottom_copy(r, c).start())

    def down_weights():
        outer_row = bottom_out[0:right, :]
        bottom_out[right : 2 * right, :] = weights(
            inner_row[...], outer_row,
            corner_left[6:7, LANES - 1 : LANES], corner_left[7:8, LANES - 1 : LANES],
            my_col == 0,
        )

    def push_down():
        push(1)
        push(2)
        push_tops(my_row + 1, near, lambda r, c: top_copy(r, c).start())

        @pl.when(has_below & jnp.logical_not(has_left))
        def _():
            push_bottoms()

    def row_line(row):
        return jnp.concatenate(
            [cells[row : row + 1, k * LANES : (k + 1) * LANES] for k in range(right)], axis=0
        )

    def col_lines(block, low, high):
        turned = [
            cells[k * LANES : (k + 1) * LANES, block * LANES : (block + 1) * LANES].T
            for k in range(down)
        ]
        return [jnp.concatenate([t[j : j + 1, :] for t in turned], axis=0) for j in range(low, high)]

    with jax.named_scope("enter_0"):
        pl.when(first)(enter)
    with jax.named_scope("load_head"):
        loads[0].wait()
    with jax.named_scope("head"):
        head_line = col_lines(0, 0, 1)[0]
        left_out[0:down, :] = head_line
        left_out[down:, :] = line_counts(head_line)
    with jax.named_scope("enter_1"):
        pl.when(between)(enter)

        @pl.when(jnp.logical_not(last))
        def _():
            push(0)

    with jax.named_scope("load_edges"):
        loads[1].wait()
        loads[2].wait()
        loads[-1].wait()
        loads[-2].wait()
    with jax.named_scope("last_row"):
        outer_row = row_line(tile_rows - 1)
        down_count = left_out[2 * down - 1 :, LANES - 1 :] - steps_down[0].astype(jnp.float32)
        bottom_out[0:right, :] = outer_row
        bottom_out[2 * right :, :] = down_count + line_counts(outer_row)
        inner_row[...] = row_line(tile_rows - 2)
        tops[my_row] = row_line(0)

        @pl.when(jnp.logical_not(has_left))
        def _():
            down_weights()

        @pl.when(jnp.logical_not(last))
        def _():
            push_down()

    lane = iota((STRIP, LANES), 1)

    def strip(k, carry):
        rows = pl.ds(pl.multiple_of(k * STRIP, STRIP), STRIP)
        wrapped_around = cells[rows, 0:LANES]
        sums = jnp.zeros((STRIP, LANES), jnp.float32)
        for j in range(right):
            cols = slice(j * LANES, (j + 1) * LANES)
            here = cells[rows, cols]
            rolled = pltpu.roll(here, 1, 1)
            across = cycles(here - jnp.where(lane == 0, wrapped_around, rolled))
            wrapped_around = rolled
            floors[rows, cols] = across.astype(jnp.bfloat16)
            sums = sums + across
        row_sums[rows, :] = sums.astype(jnp.bfloat16)
        return carry

    per_chunk = rows_step // STRIP
    for q in range(chunks):
        with jax.named_scope(f"load_{q}"):
            loads[q + 3].wait()
        with jax.named_scope(f"floors_{q}"):
            lax.fori_loop(
                q * per_chunk, (q + 1) * per_chunk, strip, 0, unroll=math.gcd(per_chunk, 8)
            )
        if q == (chunks - 1) // 2:
            with jax.named_scope("enter_2"):

                @pl.when(last)
                def _():
                    enter()
                    push(0)
                    push_down()

    with jax.named_scope("corner_left"):

        @pl.when(has_left & has_below)
        def _():
            arrived(2)
            down_weights()
            push_bottoms()

    with jax.named_scope("ends"):
        ones = jnp.ones((16, LANES), jnp.bfloat16)
        pieces = []
        for k in range(down):
            sums = lax.dot_general(
                ones, row_sums[k * LANES : (k + 1) * LANES, :], (((1,), (1,)), ((), ())),
                preferred_element_type=jnp.float32,
            )
            pieces.append(sums[0:1, :])
        end_count = left_out[down:, :] + jnp.concatenate(pieces, axis=0)
        inner_col, outer_col = col_lines(right - 1, LANES - 2, LANES)

    with jax.named_scope("halo_0"):
        arrived(0)
    with jax.named_scope("halo_1"):
        arrived(1)
    with jax.named_scope("base_h"):
        weight = weights(
            inner_col, outer_col,
            corner_above[7:8, LANES - 2 : LANES - 1], corner_above[7:8, LANES - 1 : LANES],
            my_row == 0,
        )
        across_base = mismatch(
            weight, outer_col, end_count, right_in[0:down, :], right_in[down:, :]
        ) + steps_across[0].astype(jnp.float32)
        mine_h[...] = jnp.broadcast_to(across_base, mine_h.shape)

    to_relay = jnp.where((my_row == 0) & relayed & has_right, 1, grid_rows)
    from_relay = jnp.where(has_above & relayed, my_col + 1, grid_cols)
    to_right = jnp.where(has_above & jnp.logical_not(has_left), 1, grid_cols)

    with jax.named_scope("col_in"):
        await_signals(col_in, grid_rows - near)
        along_col(near, grid_rows, lambda r, c: bottom_copy(r, c).start())
        push_tops(near, grid_rows, lambda r, c: top_copy(r, c).start())
        along_col(to_relay, grid_rows, lambda r, c: relay_in(r, c).start())

    def tell():
        with jax.named_scope("row_in"):
            known = jnp.where(has_below, my_col + 1, my_col)
            await_signals(row_in, grid_cols - 1 - known)
            along_row(my_col + 1, grid_cols, lambda r, c: row_copy(r, c).start())
        with jax.named_scope("far_in"):
            right_count = grid_cols - 1 - my_col
            await_signals(far_in, jnp.where(direct_top, (grid_rows - 1) * right_count, 0))
            far_below(lambda r, c: far_copy(r, c).start())

    def hear(slots, semaphore, first, count):
        for n in range(1, slots.shape[0]):

            @pl.when(count == n)
            def _():
                landed = slots.at[pl.ds(first, n)]
                pltpu.make_async_copy(landed, landed, semaphore).wait()

    def hear_one(ref, semaphore):
        pltpu.make_async_copy(ref, ref, semaphore).wait()

    def pass_on():
        with jax.named_scope("relay"):

            @pl.when(has_above & relayed & has_right)
            def _():
                hear_one(col_h, link_recv.at[3])
                along_row(from_relay, grid_cols, lambda r, c: relay_out(r, c).start())

        with jax.named_scope("hear_y"):
            hear(bottoms, bottom_recv, 0, my_row)
            hear(tops, top_recv, 1, my_row - 1)
        with jax.named_scope("base_y"):

            @pl.when(has_above)
            def _():
                down_here = jnp.zeros((1, 1), jnp.float32)
                for k in range(grid_rows - 1):
                    first_row = tops[k + 1]
                    value = mismatch(
                        bottoms[k, right : 2 * right, :], bottoms[k, 0:right, :],
                        bottoms[k, 2 * right :, :], first_row, line_counts(first_row),
                    )
                    down_here = down_here + jnp.where(k < my_row, value, 0.0)
                mine_y[...] = jnp.broadcast_to(down_here, mine_y.shape)
                along_row(to_right, grid_cols, lambda r, c: left_copy(r, c).start())

    def integrate():
        with jax.named_scope("integrate"):
            upper, lower = triangle(cols_step, 0), triangle(rows_step, 1)
            down_carry = jnp.zeros((1, LANES), jnp.float32)
            for q in range(chunks):
                top = q * rows_step
                rows = pl.ds(top, rows_step)
                head = cells[rows, 0:LANES]
                above = cells[max(top - 1, 0) : max(top, 1), 0:LANES]
                before = jnp.where(iota(head.shape, 0) == 0, above, pltpu.roll(head, 1, 0))
                counts = down_carry + jnp.dot(
                    lower, cycles(head - before).astype(jnp.bfloat16),
                    preferred_element_type=jnp.float32,
                )
                down_carry = counts[rows_step - 1 : rows_step, :]
                carry = counts[:, 0:1]
                for b in range(tile_cols // cols_step):
                    cols = slice(b * cols_step, (b + 1) * cols_step)
                    count = carry + jnp.dot(
                        floors[rows, cols], upper, preferred_element_type=jnp.float32
                    )
                    carry = count[:, cols_step - 1 : cols_step]
                    integ[rows, cols] = cells[rows, cols] * (1.0 / TWO_PI) - count

    tell_at = jnp.where(last, 1, 0)
    pass_at = jnp.where(has_above & relayed, 1, 2)
    integrate_at = jnp.where(last, 0, jnp.where(has_above & relayed, 2, 1))

    def phase(k, carry):
        pl.when(k == tell_at)(tell)
        pl.when(k == pass_at)(pass_on)
        pl.when(k == integrate_at)(integrate)
        return carry

    lax.fori_loop(0, 3, phase, 0)

    with jax.named_scope("sent"):
        for k in range(3):

            @pl.when(links[k][4])
            def _():
                link_copy(k).wait_send()

        push_tops(my_row + 1, grid_rows, lambda r, c: top_copy(r, c).wait_send())
        along_col(my_row + 1, grid_rows, lambda r, c: bottom_copy(r, c).wait_send())
        along_col(to_relay, grid_rows, lambda r, c: relay_in(r, c).wait_send())
        along_row(my_col + 1, grid_cols, lambda r, c: row_copy(r, c).wait_send())
        far_below(lambda r, c: far_copy(r, c).wait_send())
        along_row(from_relay, grid_cols, lambda r, c: relay_out(r, c).wait_send())
        along_row(to_right, grid_cols, lambda r, c: left_copy(r, c).wait_send())

    with jax.named_scope("hear"):
        hear(row_h, row_recv, 0, my_col)
        hear(top_h, far_recv, 0, jnp.where(has_above, my_col, 0))

        @pl.when(has_above & has_left)
        def _():
            hear_one(left_d, link_recv.at[4])

    with jax.named_scope("finish"):

        def prefix(slots):
            line = slots[0]
            for k in range(1, grid_cols):
                line = line + slots[k]
            return line

        across_here = prefix(row_h)
        across_top = jnp.where(has_above, prefix(top_h), across_here)
        down_here = mine_y[...]
        down_left = jnp.where(has_left & has_above, left_d[...], down_here)
        here = left = top = origin = zero_line
        for sweep in range(ITERS):
            prefix_across = across_here + (left - here)
            prefix_across_top = across_top + (origin - top)
            prefix_down = down_here + (top - here)
            prefix_down_left = down_left + (origin - left)
            here = here + 0.5 * (prefix_across + prefix_across_top + prefix_down + prefix_down_left)
            left = left + prefix_down_left
            top = top + prefix_across_top
        offset[...] = jnp.broadcast_to(here, offset.shape)


def place_kernel(integ, offset, out, ready, sems):
    parts = sems.shape[0]
    step = integ.shape[0] // parts
    shift = offset[0:1, 0:1]
    copies = []
    for q in range(parts):
        rows = pl.ds(q * step, step)
        ready[rows, :] = integ[rows, :] + shift
        copy = pltpu.make_async_copy(ready.at[rows], out.at[rows], sems.at[q])
        copy.start()
        copies.append(copy)
    for copy in copies:
        copy.wait()


def on_device(names, sizes, wrapped, col_steps, row_steps):
    frames, tile_rows, tile_cols = wrapped.shape
    grid_rows, grid_cols = sizes
    down, right = tile_rows // LANES, tile_cols // LANES
    dma = pltpu.SemaphoreType.DMA
    rows_step = math.gcd(tile_rows, 256)
    cols_step = math.gcd(tile_cols, 256)
    f32 = jnp.float32

    def with_local_semaphores(*refs):
        pl.run_scoped(
            functools.partial(edge_kernel, names, sizes, rows_step, cols_step, *refs),
            dma((tile_rows // rows_step + 5,)), dma((3,)), dma((grid_rows,)), dma((grid_rows,)),
            dma((grid_rows * grid_cols,)), dma((grid_rows,)), dma((grid_cols,)), dma((grid_cols,)),
        )

    call = pl.pallas_call(
        with_local_semaphores,
        out_shape=(
            pltpu.VMEM((tile_rows, tile_cols), f32),
            pltpu.VMEM((8, LANES), f32),
        ),
        in_specs=[
            pl.BlockSpec(memory_space=pltpu.HBM),
            pl.BlockSpec(memory_space=pltpu.HBM),
            pl.BlockSpec(memory_space=pltpu.HBM),
        ],
        out_specs=(
            pl.BlockSpec(memory_space=pltpu.VMEM),
            pl.BlockSpec(memory_space=pltpu.VMEM),
        ),
        scratch_shapes=[
            pltpu.VMEM((tile_rows, tile_cols), f32),
            pltpu.VMEM((2 * down, LANES), f32),
            pltpu.VMEM((2 * down, LANES), f32),
            pltpu.VMEM((8, LANES), f32),
            pltpu.VMEM((8, LANES), f32),
            pltpu.VMEM((grid_rows, right, LANES), f32),
            pltpu.VMEM((3 * right, LANES), f32),
            pltpu.VMEM((grid_rows, 3 * right, LANES), f32),
            pltpu.VMEM((right, LANES), f32),
            pltpu.VMEM((tile_rows, tile_cols), jnp.bfloat16),
            pltpu.VMEM((tile_rows, LANES), jnp.bfloat16),
            pltpu.VMEM((1, 1, 1), jnp.int32),
            pltpu.VMEM((1, 1, 1), jnp.int32),
            pltpu.VMEM((1, LANES), f32),
            pltpu.VMEM((1, LANES), f32),
            pltpu.VMEM((grid_cols, 1, LANES), f32),
            pltpu.VMEM((grid_cols, 1, LANES), f32),
            pltpu.VMEM((1, LANES), f32),
            pltpu.VMEM((1, LANES), f32),
            dma((5,)), dma, dma, dma, dma,
            pltpu.SemaphoreType.REGULAR,
            pltpu.SemaphoreType.REGULAR,
            pltpu.SemaphoreType.REGULAR,
        ],
        compiler_params=pltpu.CompilerParams(
            collective_id=0, has_side_effects=True, vmem_limit_bytes=57 * 1024 * 1024
        ),
    )
    parts = math.gcd(tile_rows // 8, 16)
    place = pl.pallas_call(
        place_kernel,
        out_shape=jax.ShapeDtypeStruct((tile_rows, tile_cols), f32),
        in_specs=[pl.BlockSpec(memory_space=pltpu.VMEM), pl.BlockSpec(memory_space=pltpu.VMEM)],
        out_specs=pl.BlockSpec(memory_space=pltpu.HBM),
        scratch_shapes=[
            pltpu.VMEM((tile_rows, tile_cols), f32),
            pltpu.SemaphoreType.DMA((parts,)),
        ],
        compiler_params=pltpu.CompilerParams(vmem_limit_bytes=24 * 1024 * 1024),
    )
    outs = [
        place(*call(wrapped[f : f + 1], col_steps[f : f + 1], row_steps[f : f + 1]))
        for f in range(frames)
    ]
    return jnp.stack(outs)


def solution(mesh):
    spec = P(None, "row", "col")
    sizes = (mesh.shape["row"], mesh.shape["col"])
    return jax.shard_map(
        functools.partial(on_device, ("row", "col"), sizes),
        mesh=mesh, in_specs=(spec, spec, spec), out_specs=spec, check_vma=False,
    )
```

time: 13.6 us -> 12 us (0.88)
  the two profiles are of different devices: /device:TPU:12 before, /device:TPU:7 now
where the time goes in v2:
time: 12 us; the launch traced here: 11.8 us
  Pallas kernels  10.5 us (88%)
  between operations  1.3 us (11%)
    pallas_call x1, Pallas kernels, on_device(): call(wrapped[f:f + 1], col_steps[f:f + 1], row_steps[f:f + 1])  8.3 us
    pallas_call x1, Pallas kernels, on_device(): place(*call(wrapped[f:f + 1], col_steps[f:f + 1], row_steps[f:f + 1]))  2.19 us

profile of v2, /device:TPU:7, one launch (start us, length us, event | category | flops | bytes accessed | tf_op | source)
XLA Modules:
  0.0 11.8 jit_solution(10826189402494106199)
XLA Ops:
  1.3 8.3 %shard_map.37 = (f32[1024,1024]{1,0:T(8,128)S(1)}, f32[8,128]{1,0:T(8,128)S(1)}) custom-call(f32[1,1024,1024]{2,1,0:T(8,128)} %refs_0_.1, s32[1,1,1]{2,1,0:T(1,128)S(6)} %copy.4.refs_1_, s32[1,1,1]{2,1,0:T(1,128)S(6)} %copy.5.refs_2_), custom_call_target="tpu_custom_call" | custom-call | tf_op jit(solution)/shard_map/pallas_call | solution.py:614
  9.6 2.2 %shard_map.38 = f32[1024,1024]{1,0:T(8,128)} custom-call(f32[1024,1024]{1,0:T(8,128)S(1)} %get-tuple-element.7.integ, f32[8,128]{1,0:T(8,128)S(1)} %get-tuple-element.8.offset), custom_call_target="tpu_custom_call" | custom-call | tf_op jit(solution)/shard_map/pallas_call | solution.py:614

commit v3 on v2

--- a/solution.py
+++ b/solution.py
@@ -13,7 +13,6 @@
 MESH = pl.DeviceIdType.MESH
 LANES = 128
 STRIP = 16
-RELAYS = 2
 
 
 def cycles(change):
@@ -80,7 +79,7 @@
     wrapped, col_steps, row_steps,
     integ, offset,
     cells, left_out, right_in, corner_above, corner_left, tops, bottom_out, bottoms, inner_row,
-    floors, row_sums, steps_across, steps_down, mine_h, mine_y, row_h, top_h, col_h, left_d,
+    floors, row_sums, steps_across, steps_down, mine_h, mine_y, row_h, top_h, col_h, left_d, carried, ends,
     link_recv, top_recv, bottom_recv, row_recv, far_recv, row_in, col_in, far_in,
     load_sem, link_send, top_send, bottom_send, h_send, c_send, t_send, d_send,
 ):
@@ -126,16 +125,23 @@
 
     has_left, has_right = my_col > 0, my_col < grid_cols - 1
     has_above, has_below = my_row > 0, my_row < grid_rows - 1
-    near = jnp.minimum(my_row + 3, grid_rows)
-    relayed = my_col < RELAYS
-    direct_top = (my_row == 0) & jnp.logical_not(relayed)
+    even_row = has_above & (lax.rem(my_row, 2) == 0)
+    tail_col = my_col >= grid_cols - 2
+    tail = (my_row == 0) & tail_col
+    unknown_above = jnp.maximum(my_row - 2, jnp.where(tail_col, jnp.minimum(my_row, 1), 0))
+    near = jnp.where(tail, my_row + 1, jnp.minimum(my_row + 3, grid_rows))
+    direct_top = (my_row == 0) & (my_col > 1)
+    first_left = jnp.where(my_row == 0, 1, 0)
+    greets_left = has_left & (has_below | (my_col == 1))
+    knows_right = has_right & (has_below | (my_col == 0))
+    pair = my_col == 1
 
     def far_below(act):
         low = jnp.where(direct_top, 1, grid_rows)
         span(low, grid_rows, lambda r: span(my_col + 1, grid_cols, lambda c: act(r, c)))
 
     def direct_tops(act):
-        span(RELAYS, jnp.where(has_above, my_col, 0), lambda c: act(0, c))
+        span(2, jnp.where(has_above, my_col, 0), lambda c: act(0, c))
 
     zero_line = jnp.zeros((1, LANES), jnp.float32)
     for slots in (row_h, top_h):
@@ -155,10 +161,11 @@
             semaphore, inc=1, device_id=(r, c), device_id_type=MESH
         )
 
-    along_row(my_col + 1, grid_cols, greet(barrier))
-    along_row(jnp.where(has_below, jnp.maximum(my_col - 1, 0), my_col), my_col, greet(barrier))
-    along_col(jnp.maximum(my_row - 2, 0), my_row, greet(barrier))
-    along_col(my_row + 3, grid_rows, greet(barrier))
+    origin = (my_row == 0) & (my_col == 0)
+    along_row(my_col + 1, jnp.where(origin, jnp.minimum(2, grid_cols), grid_cols), greet(barrier))
+    along_row(jnp.where(greets_left, my_col - 1, my_col), my_col, greet(barrier))
+    along_col(unknown_above, my_row, greet(barrier))
+    along_col(jnp.where(tail, my_row + 1, my_row + 3), grid_rows, greet(barrier))
     far_below(greet(barrier))
 
     def clear(ref, unless):
@@ -172,17 +179,23 @@
     clear(corner_left, has_left & has_below)
     clear(mine_y, has_above)
 
-    first = jnp.logical_not(has_below)
-    last = (my_row == 0) & relayed
+    first = jnp.logical_not(has_below) | tail
+    last = (my_row == 0) & (my_col < 2) & jnp.logical_not(first)
     between = jnp.logical_not(first | last)
 
     def enter():
-        sources = my_col + jnp.maximum(my_row - 2, 0)
-        sources = sources + jnp.where(has_above, jnp.maximum(my_col - RELAYS, 0), 0)
-        sources = sources + (near - 1 - my_row) + jnp.where(has_right & has_below, 1, 0)
+        sources = jnp.where(my_row == 0, jnp.where(pair, 1, jnp.maximum(my_col - 1, 0)), my_col)
+        sources = sources + unknown_above
+        sources = sources + jnp.where(has_above, jnp.maximum(my_col - 2, 0), 0)
+        sources = sources + (near - 1 - my_row) + jnp.where(knows_right, 1, 0)
         await_signals(barrier, sources)
-        along_row(0, jnp.where(has_below, my_col - 1, my_col), greet(row_in))
-        along_col(0, my_row - 2, greet(col_in))
+
+        @pl.when(jnp.logical_not(first | last))
+        def _():
+            push(0)
+
+        along_row(first_left, jnp.where(greets_left, my_col - 1, my_col), greet(row_in))
+        along_col(0, unknown_above, greet(col_in))
         direct_tops(greet(far_in))
 
     corner = cells.at[pl.ds(tile_rows - 8, 8), pl.ds(tile_cols - LANES, LANES)]
@@ -229,16 +242,19 @@
         return send(bottom_out, bottoms.at[my_row], bottom_send.at[r], bottom_recv, (r, c))
 
     def row_copy(r, c):
-        return send(mine_h, row_h.at[my_col], h_send.at[r * grid_cols + c], row_recv, (r, c))
+        return send(mine_h.at[1], row_h.at[my_col], h_send.at[r * grid_cols + c], row_recv, (r, c))
 
     def far_copy(r, c):
-        return send(mine_h, top_h.at[my_col], h_send.at[r * grid_cols + c], far_recv, (r, c))
+        return send(mine_h.at[1], top_h.at[my_col], h_send.at[r * grid_cols + c], far_recv, (r, c))
+
+    def origin_copy(r, c):
+        return send(mine_h.at[1], row_h.at[0], h_send.at[r * grid_cols + c], link_recv.at[5], (r, c))
 
     def relay_in(r, c):
         return send(mine_h, col_h, c_send.at[r], link_recv.at[3], (r, c))
 
     def relay_out(r, c):
-        return send(col_h, top_h.at[my_col], t_send.at[c], far_recv, (r, c))
+        return send(col_h.at[1], top_h.at[my_col], t_send.at[c], far_recv, (r, c))
 
     def left_copy(r, c):
         return send(mine_y, left_d, d_send.at[c], link_recv.at[4], (r, c))
@@ -258,7 +274,7 @@
         )
 
     def push_down():
-        push(1)
+        pl.when(jnp.logical_not(tail))(lambda: push(1))
         push(2)
         push_tops(my_row + 1, near, lambda r, c: top_copy(r, c).start())
 
@@ -286,12 +302,8 @@
         head_line = col_lines(0, 0, 1)[0]
         left_out[0:down, :] = head_line
         left_out[down:, :] = line_counts(head_line)
-    with jax.named_scope("enter_1"):
-        pl.when(between)(enter)
-
-        @pl.when(jnp.logical_not(last))
-        def _():
-            push(0)
+    with jax.named_scope("push_first"):
+        pl.when(first)(lambda: push(0))
 
     with jax.named_scope("load_edges"):
         loads[1].wait()
@@ -309,6 +321,9 @@
         @pl.when(jnp.logical_not(has_left))
         def _():
             down_weights()
+
+    with jax.named_scope("enter_1"):
+        pl.when(between)(enter)
 
         @pl.when(jnp.logical_not(last))
         def _():
@@ -331,8 +346,22 @@
         row_sums[rows, :] = sums.astype(jnp.bfloat16)
         return carry
 
+    def weigh_bottom():
+        arrived(2)
+        down_weights()
+        push_bottoms()
+
+    def push_further_tops():
+        await_signals(col_in, grid_rows - near)
+        pl.when(tail)(lambda: push(1))
+        push_tops(near, grid_rows, lambda r, c: top_copy(r, c).start())
+
     per_chunk = rows_step // STRIP
     for q in range(chunks):
+        if q == chunks - 1:
+            with jax.named_scope("tail_in"):
+                pl.when(tail)(push_further_tops)
+                pl.when(has_left & has_below & jnp.logical_not(last))(weigh_bottom)
         with jax.named_scope(f"load_{q}"):
             loads[q + 3].wait()
         with jax.named_scope(f"floors_{q}"):
@@ -349,55 +378,82 @@
                     push_down()
 
     with jax.named_scope("corner_left"):
-
-        @pl.when(has_left & has_below)
-        def _():
-            arrived(2)
-            down_weights()
-            push_bottoms()
-
-    with jax.named_scope("ends"):
-        ones = jnp.ones((16, LANES), jnp.bfloat16)
-        pieces = []
-        for k in range(down):
-            sums = lax.dot_general(
-                ones, row_sums[k * LANES : (k + 1) * LANES, :], (((1,), (1,)), ((), ())),
-                preferred_element_type=jnp.float32,
+        pl.when(has_left & has_below & last)(weigh_bottom)
+
+    with jax.named_scope("col_in"):
+        pl.when(jnp.logical_not(tail))(push_further_tops)
+        along_col(near, grid_rows, lambda r, c: bottom_copy(r, c).start())
+
+    to_relay = jnp.where((my_row == 0) & pair, 1, grid_rows)
+    from_relay = jnp.where(has_above & pair, my_col + 1, grid_cols)
+    to_right = jnp.where(has_above & jnp.logical_not(has_left), 1, grid_cols)
+    to_row = jnp.where(origin, grid_cols, my_col + 1)
+    paired = (my_row == 0) & pair
+
+    def hear_one(ref, semaphore):
+        pltpu.make_async_copy(ref, ref, semaphore).wait()
+
+    def across():
+        with jax.named_scope("ends"):
+            ones = jnp.ones((16, LANES), jnp.bfloat16)
+            pieces = []
+            for k in range(down):
+                sums = lax.dot_general(
+                    ones, row_sums[k * LANES : (k + 1) * LANES, :], (((1,), (1,)), ((), ())),
+                    preferred_element_type=jnp.float32,
+                )
+                pieces.append(sums[0:1, :])
+            end_count = left_out[down:, :] + jnp.concatenate(pieces, axis=0)
+            end_count = end_count - steps_across[0].astype(jnp.float32)
+            inner_col, outer_col = col_lines(right - 1, LANES - 2, LANES)
+        with jax.named_scope("halo_1"):
+            arrived(1)
+        with jax.named_scope("weights_h"):
+            weight = weights(
+                inner_col, outer_col,
+                corner_above[7:8, LANES - 2 : LANES - 1], corner_above[7:8, LANES - 1 : LANES],
+                my_row == 0,
             )
-            pieces.append(sums[0:1, :])
-        end_count = left_out[down:, :] + jnp.concatenate(pieces, axis=0)
-        inner_col, outer_col = col_lines(right - 1, LANES - 2, LANES)
-
-    with jax.named_scope("halo_0"):
-        arrived(0)
-    with jax.named_scope("halo_1"):
-        arrived(1)
-    with jax.named_scope("base_h"):
-        weight = weights(
-            inner_col, outer_col,
-            corner_above[7:8, LANES - 2 : LANES - 1], corner_above[7:8, LANES - 1 : LANES],
-            my_row == 0,
-        )
-        across_base = mismatch(
-            weight, outer_col, end_count, right_in[0:down, :], right_in[down:, :]
-        ) + steps_across[0].astype(jnp.float32)
-        mine_h[...] = jnp.broadcast_to(across_base, mine_h.shape)
-
-    to_relay = jnp.where((my_row == 0) & relayed & has_right, 1, grid_rows)
-    from_relay = jnp.where(has_above & relayed, my_col + 1, grid_cols)
-    to_right = jnp.where(has_above & jnp.logical_not(has_left), 1, grid_cols)
-
-    with jax.named_scope("col_in"):
-        await_signals(col_in, grid_rows - near)
-        along_col(near, grid_rows, lambda r, c: bottom_copy(r, c).start())
-        push_tops(near, grid_rows, lambda r, c: top_copy(r, c).start())
-        along_col(to_relay, grid_rows, lambda r, c: relay_in(r, c).start())
+            ends[0:down, :] = weight * (1.0 / summed(weight))
+            ends[down : 2 * down, :] = outer_col
+            ends[2 * down :, :] = end_count
+
+    def across_mean():
+        with jax.named_scope("halo_0"):
+            arrived(0)
+        with jax.named_scope("base_h"):
+            jump = right_in[down:, :] - ends[2 * down :, :]
+            jump = jump - cycles(right_in[0:down, :] - ends[down : 2 * down, :])
+            mine_h[1] = jnp.broadcast_to(summed(ends[0:down, :] * jump), (1, LANES))
+
+            @pl.when(paired)
+            def _():
+                hear_one(row_h.at[0], link_recv.at[5])
+                mine_h[0] = row_h[0]
+                mine_h[1] = mine_h[1] + row_h[0]
+
+            @pl.when(origin & has_right)
+            def _():
+                origin_copy(my_row, 1).start()
+
+            along_col(to_relay, grid_rows, lambda r, c: relay_in(r, c).start())
+
+    sums_first = even_row & jnp.logical_not(has_left)
+
+    def await_row():
+        known = jnp.where(knows_right, my_col + 1, my_col)
+        await_signals(row_in, jnp.where(origin, 0, grid_cols - 1 - known))
+
+    def tell_left():
+        along_row(to_right, grid_cols, lambda r, c: left_copy(r, c).start())
 
     def tell():
         with jax.named_scope("row_in"):
-            known = jnp.where(has_below, my_col + 1, my_col)
-            await_signals(row_in, grid_cols - 1 - known)
-            along_row(my_col + 1, grid_cols, lambda r, c: row_copy(r, c).start())
+            pl.when(jnp.logical_not(sums_first))(await_row)
+            along_row(to_row, grid_cols, lambda r, c: row_copy(r, c).start())
+            pl.when(jnp.logical_not(even_row))(tell_left)
+
+    def tell_far():
         with jax.named_scope("far_in"):
             right_count = grid_cols - 1 - my_col
             await_signals(far_in, jnp.where(direct_top, (grid_rows - 1) * right_count, 0))
@@ -411,17 +467,15 @@
                 landed = slots.at[pl.ds(first, n)]
                 pltpu.make_async_copy(landed, landed, semaphore).wait()
 
-    def hear_one(ref, semaphore):
-        pltpu.make_async_copy(ref, ref, semaphore).wait()
-
-    def pass_on():
+    def relay():
         with jax.named_scope("relay"):
 
-            @pl.when(has_above & relayed & has_right)
+            @pl.when(has_above & pair)
             def _():
                 hear_one(col_h, link_recv.at[3])
                 along_row(from_relay, grid_cols, lambda r, c: relay_out(r, c).start())
 
+    def down_sum():
         with jax.named_scope("hear_y"):
             hear(bottoms, bottom_recv, 0, my_row)
             hear(tops, top_recv, 1, my_row - 1)
@@ -438,13 +492,18 @@
                     )
                     down_here = down_here + jnp.where(k < my_row, value, 0.0)
                 mine_y[...] = jnp.broadcast_to(down_here, mine_y.shape)
-                along_row(to_right, grid_cols, lambda r, c: left_copy(r, c).start())
-
-    def integrate():
-        with jax.named_scope("integrate"):
+
+                @pl.when(sums_first)
+                def _():
+                    await_row()
+                    tell_left()
+
+
+    def integrate(low, high):
+        with jax.named_scope(f"integrate_{low}"):
             upper, lower = triangle(cols_step, 0), triangle(rows_step, 1)
-            down_carry = jnp.zeros((1, LANES), jnp.float32)
-            for q in range(chunks):
+            down_carry = jnp.zeros((1, LANES), jnp.float32) if low == 0 else carried[...]
+            for q in range(low, high):
                 top = q * rows_step
                 rows = pl.ds(top, rows_step)
                 head = cells[rows, 0:LANES]
@@ -463,18 +522,42 @@
                     )
                     carry = count[:, cols_step - 1 : cols_step]
                     integ[rows, cols] = cells[rows, cols] * (1.0 / TWO_PI) - count
-
-    tell_at = jnp.where(last, 1, 0)
-    pass_at = jnp.where(has_above & relayed, 1, 2)
-    integrate_at = jnp.where(last, 0, jnp.where(has_above & relayed, 2, 1))
+            if high < chunks:
+                carried[...] = down_carry
+
+    left_side = has_above & jnp.logical_not(has_left)
+    split = (even_row & has_left) | (tail_col & (my_row == 1))
+    half = (chunks + 1) // 2
+    left_odd, left_even, paired_at, split_at, otherwise = range(5)
+    never = 8
+    kind = jnp.where(pair, paired_at, jnp.where(split, split_at, otherwise))
+    kind = jnp.where(left_side, jnp.where(even_row, left_even, left_odd), kind)
+
+    def pick(*slots):
+        chosen = slots[otherwise]
+        for k in range(otherwise):
+            chosen = jnp.where(kind == k, slots[k], chosen)
+        return chosen
+
+    order = (
+        (across, jnp.where(has_right, pick(0, 1, 1, 1, 0), never)),
+        (across_mean, jnp.where(has_right, pick(1, 3, 2, 2, 1), never)),
+        (tell, pick(3, 4, 3, 3, 2)),
+        (functools.partial(integrate, 0, half), pick(4, 0, 0, 0, 3)),
+        (tell_far, jnp.where(direct_top, 4, never)),
+        (functools.partial(integrate, half, chunks), pick(5, 5, 6, 4, 5)),
+        (down_sum, pick(2, 2, jnp.where(even_row, 5, 4), 5, 6)),
+        (relay, pick(6, 6, jnp.where(even_row, 4, 5), 6, 6)),
+    )
 
     def phase(k, carry):
-        pl.when(k == tell_at)(tell)
-        pl.when(k == pass_at)(pass_on)
-        pl.when(k == integrate_at)(integrate)
+        for act, at in order:
+            pl.when(k == at)(act)
         return carry
 
-    lax.fori_loop(0, 3, phase, 0)
+    lax.fori_loop(0, len(order), phase, 0)
+
+    pl.when(jnp.logical_not(has_right))(lambda: arrived(1))
 
     with jax.named_scope("sent"):
         for k in range(3):
@@ -486,14 +569,20 @@
         push_tops(my_row + 1, grid_rows, lambda r, c: top_copy(r, c).wait_send())
         along_col(my_row + 1, grid_rows, lambda r, c: bottom_copy(r, c).wait_send())
         along_col(to_relay, grid_rows, lambda r, c: relay_in(r, c).wait_send())
-        along_row(my_col + 1, grid_cols, lambda r, c: row_copy(r, c).wait_send())
+        along_row(to_row, grid_cols, lambda r, c: row_copy(r, c).wait_send())
+
+        @pl.when(origin & has_right)
+        def _():
+            origin_copy(my_row, 1).wait_send()
+
         far_below(lambda r, c: far_copy(r, c).wait_send())
         along_row(from_relay, grid_cols, lambda r, c: relay_out(r, c).wait_send())
         along_row(to_right, grid_cols, lambda r, c: left_copy(r, c).wait_send())
 
     with jax.named_scope("hear"):
-        hear(row_h, row_recv, 0, my_col)
-        hear(top_h, far_recv, 0, jnp.where(has_above, my_col, 0))
+        hear(row_h, row_recv, 1, jnp.where(has_above, 0, my_col - 1))
+        hear(row_h, row_recv, 0, jnp.where(has_above, my_col, 0))
+        hear(top_h, far_recv, 1, jnp.where(has_above, my_col - 1, 0))
 
         @pl.when(has_above & has_left)
         def _():
@@ -508,15 +597,16 @@
             return line
 
         across_here = prefix(row_h)
-        across_top = jnp.where(has_above, prefix(top_h), across_here)
+        across_top = jnp.where(pair, col_h[0], prefix(top_h))
+        across_top = jnp.where(has_above, across_top, across_here)
         down_here = mine_y[...]
         down_left = jnp.where(has_left & has_above, left_d[...], down_here)
-        here = left = top = origin = zero_line
+        here = left = top = start = zero_line
         for sweep in range(ITERS):
             prefix_across = across_here + (left - here)
-            prefix_across_top = across_top + (origin - top)
+            prefix_across_top = across_top + (start - top)
             prefix_down = down_here + (top - here)
-            prefix_down_left = down_left + (origin - left)
+            prefix_down_left = down_left + (start - left)
             here = here + 0.5 * (prefix_across + prefix_across_top + prefix_down + prefix_down_left)
             left = left + prefix_down_left
             top = top + prefix_across_top
@@ -583,13 +673,15 @@
             pltpu.VMEM((tile_rows, LANES), jnp.bfloat16),
             pltpu.VMEM((1, 1, 1), jnp.int32),
             pltpu.VMEM((1, 1, 1), jnp.int32),
-            pltpu.VMEM((1, LANES), f32),
+            pltpu.VMEM((2, 1, LANES), f32),
             pltpu.VMEM((1, LANES), f32),
             pltpu.VMEM((grid_cols, 1, LANES), f32),
             pltpu.VMEM((grid_cols, 1, LANES), f32),
+            pltpu.VMEM((2, 1, LANES), f32),
             pltpu.VMEM((1, LANES), f32),
             pltpu.VMEM((1, LANES), f32),
-            dma((5,)), dma, dma, dma, dma,
+            pltpu.VMEM((3 * down, LANES), f32),
+            dma((6,)), dma, dma, dma, dma,
             pltpu.SemaphoreType.REGULAR,
             pltpu.SemaphoreType.REGULAR,
             pltpu.SemaphoreType.REGULAR,

time: 12 us -> 11.3 us (0.942)
  the two profiles are of different devices: /device:TPU:7 before, /device:TPU:12 now
where the time goes in v3:
time: 11.3 us; the launch traced here: 11.1 us
  Pallas kernels  9.81 us (87%)
  between operations  1.3 us (12%)
    pallas_call x1, Pallas kernels, on_device(): call(wrapped[f:f + 1], col_steps[f:f + 1], row_steps[f:f + 1])  7.62 us
    pallas_call x1, Pallas kernels, on_device(): place(*call(wrapped[f:f + 1], col_steps[f:f + 1], row_steps[f:f + 1]))  2.19 us

profile of v3, /device:TPU:12, one launch (start us, length us, event | category | flops | bytes accessed | tf_op | source)
XLA Modules:
  0.0 11.1 jit_solution(6759563223922048901)
XLA Ops:
  1.3 7.6 %shard_map.37 = (f32[1024,1024]{1,0:T(8,128)S(1)}, f32[8,128]{1,0:T(8,128)S(1)}) custom-call(f32[1,1024,1024]{2,1,0:T(8,128)} %refs_0_.1, s32[1,1,1]{2,1,0:T(1,128)S(6)} %copy.4.refs_1_, s32[1,1,1]{2,1,0:T(1,128)S(6)} %copy.5.refs_2_), custom_call_target="tpu_custom_call" | custom-call | tf_op jit(solution)/shard_map/pallas_call | solution.py:706
  8.9 2.2 %shard_map.38 = f32[1024,1024]{1,0:T(8,128)} custom-call(f32[1024,1024]{1,0:T(8,128)S(1)} %get-tuple-element.7.integ, f32[8,128]{1,0:T(8,128)S(1)} %get-tuple-element.8.offset), custom_call_target="tpu_custom_call" | custom-call | tf_op jit(solution)/shard_map/pallas_call | solution.py:706

commit v4 on v3

--- a/solution.py
+++ b/solution.py
@@ -79,9 +79,9 @@
     wrapped, col_steps, row_steps,
     integ, offset,
     cells, left_out, right_in, corner_above, corner_left, tops, bottom_out, bottoms, inner_row,
-    floors, row_sums, steps_across, steps_down, mine_h, mine_y, row_h, top_h, col_h, left_d, carried, ends,
+    floors, row_sums, steps_across, steps_down, mine_h, mine_y, row_h, top_h, col_h, left_d, carried, ends, ends_in, pair_in, first_inner, left_sums,
     link_recv, top_recv, bottom_recv, row_recv, far_recv, row_in, col_in, far_in,
-    load_sem, link_send, top_send, bottom_send, h_send, c_send, t_send, d_send,
+    load_sem, link_send, top_send, bottom_send, h_send, c_send, d_send,
 ):
     row_name, col_name = names
     grid_rows, grid_cols = sizes
@@ -105,10 +105,12 @@
         loads.append(
             pltpu.make_async_copy(wrapped.at[0, rows, cols], cells.at[rows, cols], load_sem.at[k])
         )
-        loads[-1].start()
     for source, target in ((col_steps, steps_across), (row_steps, steps_down)):
         loads.append(pltpu.make_async_copy(source, target, load_sem.at[len(loads)]))
-        loads[-1].start()
+
+    def start_loads():
+        for load in loads:
+            load.start()
 
     def span(low, high, act):
         def step(k, carry):
@@ -127,27 +129,38 @@
     has_above, has_below = my_row > 0, my_row < grid_rows - 1
     even_row = has_above & (lax.rem(my_row, 2) == 0)
     tail_col = my_col >= grid_cols - 2
-    tail = (my_row == 0) & tail_col
-    unknown_above = jnp.maximum(my_row - 2, jnp.where(tail_col, jnp.minimum(my_row, 1), 0))
+    tail = tail_col & has_below & (lax.rem(my_row, 2) == 0)
+
+    def unknown_to(row):
+        return (row < my_row) & ((my_row - row > 2) | (tail_col & (lax.rem(row, 2) == 0)))
+
+    unknown_above = sum(jnp.where(unknown_to(k), 1, 0) for k in range(grid_rows))
     near = jnp.where(tail, my_row + 1, jnp.minimum(my_row + 3, grid_rows))
-    direct_top = (my_row == 0) & (my_col > 1)
-    first_left = jnp.where(my_row == 0, 1, 0)
-    greets_left = has_left & (has_below | (my_col == 1))
-    knows_right = has_right & (has_below | (my_col == 0))
+    direct_top = (my_row == 0) & (my_col > 2)
+    first_left = jnp.where(my_row == 0, 3, 0)
+    lead = (my_row == 0) & (my_col < 3)
     pair = my_col == 1
+    paired = (my_row == 0) & pair
+    second = (my_row == 0) & (my_col == 3)
+    before_second = (my_row == 0) & (my_col == 2)
+    greets_left = has_left & (has_below | pair | second | before_second)
+    knows_right = has_right & (has_below | (my_col == 0) | paired | before_second)
 
     def far_below(act):
         low = jnp.where(direct_top, 1, grid_rows)
         span(low, grid_rows, lambda r: span(my_col + 1, grid_cols, lambda c: act(r, c)))
 
+    def left_below(act):
+        span(jnp.where(second, 1, grid_rows), grid_rows, lambda r: act(r, my_col - 1))
+
     def direct_tops(act):
-        span(2, jnp.where(has_above, my_col, 0), lambda c: act(0, c))
+        span(3, jnp.where(has_above, my_col, 0), lambda c: act(0, c))
+
+        @pl.when(has_above & (my_col == 2))
+        def _():
+            act(0, 3)
 
     zero_line = jnp.zeros((1, LANES), jnp.float32)
-    for slots in (row_h, top_h):
-        for k in range(grid_cols):
-            slots[k] = zero_line
-
     barrier = pltpu.get_barrier_semaphore()
 
     def await_signals(semaphore, count):
@@ -162,11 +175,36 @@
         )
 
     origin = (my_row == 0) & (my_col == 0)
-    along_row(my_col + 1, jnp.where(origin, jnp.minimum(2, grid_cols), grid_cols), greet(barrier))
+
+    def greet_above(semaphore, unknown):
+
+        def greet_row(r, c):
+
+            @pl.when(unknown_to(r) == unknown)
+            def _():
+                greet(semaphore)(r, c)
+
+        along_col(0 if unknown else jnp.maximum(my_row - 2, 0), my_row, greet_row)
+
+    for slots in (row_h, top_h):
+        for k in range(grid_cols):
+            slots[k] = zero_line
+
+    greet_above(barrier, False)
     along_row(jnp.where(greets_left, my_col - 1, my_col), my_col, greet(barrier))
-    along_col(unknown_above, my_row, greet(barrier))
+    start_loads()
+    pair_top = (my_row == 0) & (my_col < 2)
+    few = my_col + jnp.where(paired, 1, 2)
+    along_row(my_col + 1, jnp.where(lead, few, grid_cols), greet(barrier))
+
+    @pl.when(second)
+    def _():
+        greet(barrier)(0, 0)
+        greet(barrier)(0, 1)
+
     along_col(jnp.where(tail, my_row + 1, my_row + 3), grid_rows, greet(barrier))
     far_below(greet(barrier))
+    left_below(greet(barrier))
 
     def clear(ref, unless):
 
@@ -183,26 +221,34 @@
     last = (my_row == 0) & (my_col < 2) & jnp.logical_not(first)
     between = jnp.logical_not(first | last)
 
+    weighs_late = last | before_second
+
     def enter():
-        sources = jnp.where(my_row == 0, jnp.where(pair, 1, jnp.maximum(my_col - 1, 0)), my_col)
+        top_sources = jnp.where(paired | second, 1, jnp.maximum(my_col - 3, 0))
+        sources = jnp.where(my_row == 0, top_sources, my_col)
+        sources = sources + jnp.where(pair_top, 1, 0)
         sources = sources + unknown_above
-        sources = sources + jnp.where(has_above, jnp.maximum(my_col - 2, 0), 0)
+        sources = sources + jnp.where(has_above, jnp.maximum(my_col - 3, 0), 0)
+        sources = sources + jnp.where(has_above & (my_col == 2), 1, 0)
         sources = sources + (near - 1 - my_row) + jnp.where(knows_right, 1, 0)
         await_signals(barrier, sources)
 
         @pl.when(jnp.logical_not(first | last))
         def _():
             push(0)
+            push(4)
 
         along_row(first_left, jnp.where(greets_left, my_col - 1, my_col), greet(row_in))
-        along_col(0, unknown_above, greet(col_in))
+        greet_above(col_in, True)
         direct_tops(greet(far_in))
 
     corner = cells.at[pl.ds(tile_rows - 8, 8), pl.ds(tile_cols - LANES, LANES)]
     links = (
-        (left_out, right_in, 0, -1, has_left, has_right),
+        (left_out, right_in, 0, -1, has_left & jnp.logical_not(before_second), has_right & jnp.logical_not(paired)),
         (corner, corner_above, 1, 0, has_below, has_above),
         (corner, corner_left, 0, 1, has_right & has_below, has_left & has_below),
+        (ends, ends_in, 0, 2, paired, second),
+        (left_out, pair_in, 0, 1, before_second, second),
     )
 
     def link_copy(k):
@@ -251,13 +297,16 @@
         return send(mine_h.at[1], row_h.at[0], h_send.at[r * grid_cols + c], link_recv.at[5], (r, c))
 
     def relay_in(r, c):
-        return send(mine_h, col_h, c_send.at[r], link_recv.at[3], (r, c))
-
-    def relay_out(r, c):
-        return send(col_h.at[1], top_h.at[my_col], t_send.at[c], far_recv, (r, c))
+        return send(mine_h.at[2], col_h, c_send.at[r], link_recv.at[6], (r, c))
+
+    def relay_left(r, c):
+        return send(mine_h.at[0], col_h, h_send.at[r * grid_cols + c], link_recv.at[6], (r, c))
+
+    def relay_back(r, c):
+        return send(mine_h.at[0], row_h.at[1], h_send.at[r * grid_cols + c], link_recv.at[5], (r, c))
 
     def left_copy(r, c):
-        return send(mine_y, left_d, d_send.at[c], link_recv.at[4], (r, c))
+        return send(mine_y, left_d, d_send.at[c], link_recv.at[7], (r, c))
 
     def push_tops(low, high, act):
         along_col(jnp.where(has_above, low, grid_rows), high, act)
@@ -276,7 +325,6 @@
     def push_down():
         pl.when(jnp.logical_not(tail))(lambda: push(1))
         push(2)
-        push_tops(my_row + 1, near, lambda r, c: top_copy(r, c).start())
 
         @pl.when(has_below & jnp.logical_not(has_left))
         def _():
@@ -303,7 +351,12 @@
         left_out[0:down, :] = head_line
         left_out[down:, :] = line_counts(head_line)
     with jax.named_scope("push_first"):
-        pl.when(first)(lambda: push(0))
+
+        @pl.when(first)
+        def _():
+            push(0)
+            push(4)
+
 
     with jax.named_scope("load_edges"):
         loads[1].wait()
@@ -316,7 +369,6 @@
         bottom_out[0:right, :] = outer_row
         bottom_out[2 * right :, :] = down_count + line_counts(outer_row)
         inner_row[...] = row_line(tile_rows - 2)
-        tops[my_row] = row_line(0)
 
         @pl.when(jnp.logical_not(has_left))
         def _():
@@ -328,6 +380,16 @@
         @pl.when(jnp.logical_not(last))
         def _():
             push_down()
+
+    with jax.named_scope("first_row"):
+
+        @pl.when(has_above)
+        def _():
+            first_row = row_line(0)
+            tops[my_row, 0:right, :] = first_row
+            tops[my_row, right:, :] = line_counts(first_row)
+
+        push_tops(my_row + 1, near, lambda r, c: top_copy(r, c).start())
 
     lane = iota((STRIP, LANES), 1)
 
@@ -361,7 +423,7 @@
         if q == chunks - 1:
             with jax.named_scope("tail_in"):
                 pl.when(tail)(push_further_tops)
-                pl.when(has_left & has_below & jnp.logical_not(last))(weigh_bottom)
+                pl.when(has_left & has_below & jnp.logical_not(weighs_late))(weigh_bottom)
         with jax.named_scope(f"load_{q}"):
             loads[q + 3].wait()
         with jax.named_scope(f"floors_{q}"):
@@ -378,22 +440,26 @@
                     push_down()
 
     with jax.named_scope("corner_left"):
-        pl.when(has_left & has_below & last)(weigh_bottom)
+        pl.when(has_left & has_below & weighs_late)(weigh_bottom)
 
     with jax.named_scope("col_in"):
         pl.when(jnp.logical_not(tail))(push_further_tops)
         along_col(near, grid_rows, lambda r, c: bottom_copy(r, c).start())
 
-    to_relay = jnp.where((my_row == 0) & pair, 1, grid_rows)
-    from_relay = jnp.where(has_above & pair, my_col + 1, grid_cols)
-    to_right = jnp.where(has_above & jnp.logical_not(has_left), 1, grid_cols)
-    to_row = jnp.where(origin, grid_cols, my_col + 1)
-    paired = (my_row == 0) & pair
+    relays = (my_col > 0) & (my_col < 4)
+    to_relay = jnp.where(paired | second, 1, grid_rows)
+    left_side = has_above & jnp.logical_not(has_left)
+    to_right = jnp.where(left_side, 1, grid_cols)
+    to_row = jnp.where(pair_top, grid_cols, my_col + 1)
+    row_end = jnp.where(before_second, 4, grid_cols)
+
+    def pair_places(act):
+        span(jnp.where(origin, 0, 2), 2, lambda k: act(0, 1 + 2 * k))
 
     def hear_one(ref, semaphore):
         pltpu.make_async_copy(ref, ref, semaphore).wait()
 
-    def across():
+    def end_values():
         with jax.named_scope("ends"):
             ones = jnp.ones((16, LANES), jnp.bfloat16)
             pieces = []
@@ -405,99 +471,145 @@
                 pieces.append(sums[0:1, :])
             end_count = left_out[down:, :] + jnp.concatenate(pieces, axis=0)
             end_count = end_count - steps_across[0].astype(jnp.float32)
-            inner_col, outer_col = col_lines(right - 1, LANES - 2, LANES)
-        with jax.named_scope("halo_1"):
-            arrived(1)
+            return (end_count, *col_lines(right - 1, LANES - 2, LANES))
+
+    def rest_weights(inner_col, outer_col):
+        weight = weights(inner_col, outer_col, inner_col[0:1, 0:1], outer_col[0:1, 0:1], True)
+        start = (iota(weight.shape, 0) == 0) & (iota(weight.shape, 1) == 0)
+        return jnp.where(start & has_above, 0.0, weight)
+
+    def first_weight(inner, outer):
+        inner_before = corner_above[7:8, LANES - 2 : LANES - 1]
+        outer_before = corner_above[7:8, LANES - 1 : LANES]
+        charge = cycles(outer_before - inner_before) + cycles(outer - outer_before)
+        charge = charge - cycles(outer - inner) - cycles(inner - inner_before)
+        return jnp.where(has_above, 1.0 / (1.0 + jnp.abs(charge)), 0.0)
+
+    def end_sums(weight, outer_col, end_count, first_col, first_count):
+        jump = first_count - end_count - cycles(first_col - outer_col)
+        return summed(weight * jump), summed(weight), jump[0:1, 0:1]
+
+    def finish_mean(sums, inner, outer):
+        jumps, weight, first_jump = sums
+        extra = first_weight(inner, outer)
+        return jnp.broadcast_to((jumps + extra * first_jump) / (weight + extra), (1, LANES))
+
+    def across():
+        end_count, inner_col, outer_col = end_values()
         with jax.named_scope("weights_h"):
-            weight = weights(
-                inner_col, outer_col,
-                corner_above[7:8, LANES - 2 : LANES - 1], corner_above[7:8, LANES - 1 : LANES],
-                my_row == 0,
-            )
-            ends[0:down, :] = weight * (1.0 / summed(weight))
+            ends[0:down, :] = rest_weights(inner_col, outer_col)
             ends[down : 2 * down, :] = outer_col
             ends[2 * down :, :] = end_count
+            first_inner[...] = inner_col[0:1, :]
+            push(3)
 
     def across_mean():
         with jax.named_scope("halo_0"):
             arrived(0)
         with jax.named_scope("base_h"):
-            jump = right_in[down:, :] - ends[2 * down :, :]
-            jump = jump - cycles(right_in[0:down, :] - ends[down : 2 * down, :])
-            mine_h[1] = jnp.broadcast_to(summed(ends[0:down, :] * jump), (1, LANES))
+            sums = end_sums(
+                ends[0:down, :], ends[down : 2 * down, :], ends[2 * down :, :],
+                right_in[0:down, :], right_in[down:, :],
+            )
+            arrived(1)
+            mine_h[1] = finish_mean(sums, first_inner[0:1, 0:1], ends[down : down + 1, 0:1])
+            pair_places(lambda r, c: origin_copy(r, c).start())
+
+    def across_pair():
+        with jax.named_scope("pair"):
+            hear_one(row_h.at[0], link_recv.at[5])
 
             @pl.when(paired)
             def _():
-                hear_one(row_h.at[0], link_recv.at[5])
-                mine_h[0] = row_h[0]
-                mine_h[1] = mine_h[1] + row_h[0]
-
-            @pl.when(origin & has_right)
+                mine_h[2] = row_h[0]
+
+            @pl.when(second)
             def _():
-                origin_copy(my_row, 1).start()
+                arrived(4)
+                hear_one(row_h.at[2], row_recv)
+                arrived(3)
+                jumps, weight, _ = end_sums(
+                    ends_in[0:down, :], ends_in[down : 2 * down, :], ends_in[2 * down :, :],
+                    pair_in[0:down, :], pair_in[down:, :],
+                )
+                before = jnp.broadcast_to(jumps / weight, (1, LANES))
+                row_h[1] = before
+                upto = row_h[0] + before
+                mine_h[0] = upto
+                mine_h[2] = upto + row_h[2]
+                mine_h[1] = mine_h[1] + (upto + row_h[2])
+                relay_back(0, 2).start()
 
             along_col(to_relay, grid_rows, lambda r, c: relay_in(r, c).start())
-
-    sums_first = even_row & jnp.logical_not(has_left)
 
     def await_row():
         known = jnp.where(knows_right, my_col + 1, my_col)
-        await_signals(row_in, jnp.where(origin, 0, grid_cols - 1 - known))
-
-    def tell_left():
-        along_row(to_right, grid_cols, lambda r, c: left_copy(r, c).start())
+        await_signals(row_in, jnp.where(lead, 0, grid_cols - 1 - known))
 
     def tell():
         with jax.named_scope("row_in"):
-            pl.when(jnp.logical_not(sums_first))(await_row)
-            along_row(to_row, grid_cols, lambda r, c: row_copy(r, c).start())
-            pl.when(jnp.logical_not(even_row))(tell_left)
+            await_row()
+            along_row(to_row, row_end, lambda r, c: row_copy(r, c).start())
 
     def tell_far():
         with jax.named_scope("far_in"):
-            right_count = grid_cols - 1 - my_col
+            right_count = grid_cols - 1 - my_col + jnp.where(second, 1, 0)
             await_signals(far_in, jnp.where(direct_top, (grid_rows - 1) * right_count, 0))
+            left_below(lambda r, c: relay_left(r, c).start())
             far_below(lambda r, c: far_copy(r, c).start())
 
     def hear(slots, semaphore, first, count):
-        for n in range(1, slots.shape[0]):
+        for n in range(1, slots.shape[0] - max(first - 1, 0)):
 
             @pl.when(count == n)
             def _():
                 landed = slots.at[pl.ds(first, n)]
                 pltpu.make_async_copy(landed, landed, semaphore).wait()
 
-    def relay():
-        with jax.named_scope("relay"):
-
-            @pl.when(has_above & pair)
-            def _():
-                hear_one(col_h, link_recv.at[3])
-                along_row(from_relay, grid_cols, lambda r, c: relay_out(r, c).start())
+    def hear_above():
+        with jax.named_scope("hear_y"):
+            hear(tops, top_recv, 1, my_row - 1)
+            hear(bottoms, bottom_recv, 0, my_row)
+
+    def sum_above():
+        down_here = jnp.zeros((1, 1), jnp.float32)
+        for k in range(grid_rows - 1):
+            value = mismatch(
+                bottoms[k, right : 2 * right, :], bottoms[k, 0:right, :],
+                bottoms[k, 2 * right :, :], tops[k + 1, 0:right, :], tops[k + 1, right:, :],
+            )
+            down_here = down_here + jnp.where(k < my_row, value, 0.0)
+        mine_y[...] = jnp.broadcast_to(down_here, mine_y.shape)
 
     def down_sum():
-        with jax.named_scope("hear_y"):
-            hear(bottoms, bottom_recv, 0, my_row)
-            hear(tops, top_recv, 1, my_row - 1)
+        hear_above()
         with jax.named_scope("base_y"):
-
-            @pl.when(has_above)
-            def _():
-                down_here = jnp.zeros((1, 1), jnp.float32)
-                for k in range(grid_rows - 1):
-                    first_row = tops[k + 1]
-                    value = mismatch(
-                        bottoms[k, right : 2 * right, :], bottoms[k, 0:right, :],
-                        bottoms[k, 2 * right :, :], first_row, line_counts(first_row),
-                    )
-                    down_here = down_here + jnp.where(k < my_row, value, 0.0)
-                mine_y[...] = jnp.broadcast_to(down_here, mine_y.shape)
-
-                @pl.when(sums_first)
-                def _():
-                    await_row()
-                    tell_left()
-
+            pl.when(has_above)(sum_above)
+
+    def left_start():
+        end_count, inner_col, outer_col = end_values()
+        with jax.named_scope("halo_left"):
+            arrived(0)
+        with jax.named_scope("weights_left"):
+            sums = end_sums(
+                rest_weights(inner_col, outer_col), outer_col, end_count,
+                right_in[0:down, :], right_in[down:, :],
+            )
+            for k, value in enumerate((*sums, inner_col[0:1, 0:1], outer_col[0:1, 0:1])):
+                left_sums[k] = jnp.broadcast_to(value, (1, LANES))
+
+    def left_finish():
+        with jax.named_scope("halo_left_1"):
+            arrived(1)
+            jumps, weight, jump, inner, outer = (left_sums[k] for k in range(5))
+            mine_h[1] = finish_mean((jumps, weight, jump), inner, outer)
+        hear_above()
+        with jax.named_scope("base_left"):
+            sum_above()
+        with jax.named_scope("row_in_left"):
+            await_row()
+            along_row(to_right, grid_cols, lambda r, c: left_copy(r, c).start())
+            along_row(to_row, row_end, lambda r, c: row_copy(r, c).start())
 
     def integrate(low, high):
         with jax.named_scope(f"integrate_{low}"):
@@ -525,13 +637,15 @@
             if high < chunks:
                 carried[...] = down_carry
 
-    left_side = has_above & jnp.logical_not(has_left)
-    split = (even_row & has_left) | (tail_col & (my_row == 1))
+    odd_row = lax.rem(my_row, 2) == 1
+    far_early = (my_row == 0) & (my_col > 3)
+    split = (even_row & has_left) | (tail_col & odd_row)
     half = (chunks + 1) // 2
-    left_odd, left_even, paired_at, split_at, otherwise = range(5)
-    never = 8
-    kind = jnp.where(pair, paired_at, jnp.where(split, split_at, otherwise))
-    kind = jnp.where(left_side, jnp.where(even_row, left_even, left_odd), kind)
+    never = 10
+    at_left, at_top, at_pair, at_split, at_second, otherwise = range(6)
+    kind = jnp.where(second, at_second, jnp.where(split, at_split, otherwise))
+    kind = jnp.where(pair, jnp.where(paired, at_top, at_pair), kind)
+    kind = jnp.where(left_side, at_left, kind)
 
     def pick(*slots):
         chosen = slots[otherwise]
@@ -540,14 +654,16 @@
         return chosen
 
     order = (
-        (across, jnp.where(has_right, pick(0, 1, 1, 1, 0), never)),
-        (across_mean, jnp.where(has_right, pick(1, 3, 2, 2, 1), never)),
-        (tell, pick(3, 4, 3, 3, 2)),
-        (functools.partial(integrate, 0, half), pick(4, 0, 0, 0, 3)),
-        (tell_far, jnp.where(direct_top, 4, never)),
-        (functools.partial(integrate, half, chunks), pick(5, 5, 6, 4, 5)),
-        (down_sum, pick(2, 2, jnp.where(even_row, 5, 4), 5, 6)),
-        (relay, pick(6, 6, jnp.where(even_row, 4, 5), 6, 6)),
+        (left_start, pick(0, never, never, never, never, never)),
+        (left_finish, pick(2, never, never, never, never, never)),
+        (across, jnp.where(has_right, pick(never, 0, 1, 1, 1, 0), never)),
+        (across_mean, jnp.where(has_right, pick(never, never, 2, 2, 2, 1), never)),
+        (across_pair, pick(never, 2, never, never, 3, never)),
+        (tell, pick(never, never, 3, 3, 4, 2)),
+        (functools.partial(integrate, 0, half), pick(1, 1, 0, 0, 0, jnp.where(far_early, 4, 3))),
+        (tell_far, jnp.where(direct_top, jnp.where(second, 5, jnp.where(far_early, 3, 4)), never)),
+        (functools.partial(integrate, half, chunks), pick(3, 3, 5, 4, 6, 5)),
+        (down_sum, pick(never, never, 4, 5, never, 6)),
     )
 
     def phase(k, carry):
@@ -557,10 +673,10 @@
 
     lax.fori_loop(0, len(order), phase, 0)
 
-    pl.when(jnp.logical_not(has_right))(lambda: arrived(1))
+    pl.when(jnp.logical_not(has_right | left_side))(lambda: arrived(1))
 
     with jax.named_scope("sent"):
-        for k in range(3):
+        for k in range(5):
 
             @pl.when(links[k][4])
             def _():
@@ -569,24 +685,33 @@
         push_tops(my_row + 1, grid_rows, lambda r, c: top_copy(r, c).wait_send())
         along_col(my_row + 1, grid_rows, lambda r, c: bottom_copy(r, c).wait_send())
         along_col(to_relay, grid_rows, lambda r, c: relay_in(r, c).wait_send())
-        along_row(to_row, grid_cols, lambda r, c: row_copy(r, c).wait_send())
-
-        @pl.when(origin & has_right)
-        def _():
-            origin_copy(my_row, 1).wait_send()
+        along_row(to_row, row_end, lambda r, c: row_copy(r, c).wait_send())
+        pair_places(lambda r, c: origin_copy(r, c).wait_send())
+        left_below(lambda r, c: relay_left(r, c).wait_send())
+
+        @pl.when(second)
+        def _():
+            relay_back(0, 2).wait_send()
 
         far_below(lambda r, c: far_copy(r, c).wait_send())
-        along_row(from_relay, grid_cols, lambda r, c: relay_out(r, c).wait_send())
         along_row(to_right, grid_cols, lambda r, c: left_copy(r, c).wait_send())
 
     with jax.named_scope("hear"):
-        hear(row_h, row_recv, 1, jnp.where(has_above, 0, my_col - 1))
+        hear(row_h, row_recv, 3, jnp.where(has_above, 0, my_col - 3))
         hear(row_h, row_recv, 0, jnp.where(has_above, my_col, 0))
-        hear(top_h, far_recv, 1, jnp.where(has_above, my_col - 1, 0))
+        hear(top_h, far_recv, 3, jnp.where(has_above, my_col - 3, 0))
+
+        @pl.when(has_above & relays)
+        def _():
+            hear_one(col_h, link_recv.at[6])
+
+        @pl.when(before_second)
+        def _():
+            hear_one(row_h.at[1], link_recv.at[5])
 
         @pl.when(has_above & has_left)
         def _():
-            hear_one(left_d, link_recv.at[4])
+            hear_one(left_d, link_recv.at[7])
 
     with jax.named_scope("finish"):
 
@@ -597,7 +722,7 @@
             return line
 
         across_here = prefix(row_h)
-        across_top = jnp.where(pair, col_h[0], prefix(top_h))
+        across_top = prefix(top_h) + jnp.where(relays, col_h[...], 0.0)
         across_top = jnp.where(has_above, across_top, across_here)
         down_here = mine_y[...]
         down_left = jnp.where(has_left & has_above, left_d[...], down_here)
@@ -640,8 +765,8 @@
     def with_local_semaphores(*refs):
         pl.run_scoped(
             functools.partial(edge_kernel, names, sizes, rows_step, cols_step, *refs),
-            dma((tile_rows // rows_step + 5,)), dma((3,)), dma((grid_rows,)), dma((grid_rows,)),
-            dma((grid_rows * grid_cols,)), dma((grid_rows,)), dma((grid_cols,)), dma((grid_cols,)),
+            dma((tile_rows // rows_step + 5,)), dma((5,)), dma((grid_rows,)), dma((grid_rows,)),
+            dma((grid_rows * grid_cols,)), dma((grid_rows,)), dma((grid_cols,)),
         )
 
     call = pl.pallas_call(
@@ -665,7 +790,7 @@
             pltpu.VMEM((2 * down, LANES), f32),
             pltpu.VMEM((8, LANES), f32),
             pltpu.VMEM((8, LANES), f32),
-            pltpu.VMEM((grid_rows, right, LANES), f32),
+            pltpu.VMEM((grid_rows, 2 * right, LANES), f32),
             pltpu.VMEM((3 * right, LANES), f32),
             pltpu.VMEM((grid_rows, 3 * right, LANES), f32),
             pltpu.VMEM((right, LANES), f32),
@@ -673,15 +798,19 @@
             pltpu.VMEM((tile_rows, LANES), jnp.bfloat16),
             pltpu.VMEM((1, 1, 1), jnp.int32),
             pltpu.VMEM((1, 1, 1), jnp.int32),
-            pltpu.VMEM((2, 1, LANES), f32),
+            pltpu.VMEM((3, 1, LANES), f32),
             pltpu.VMEM((1, LANES), f32),
             pltpu.VMEM((grid_cols, 1, LANES), f32),
             pltpu.VMEM((grid_cols, 1, LANES), f32),
-            pltpu.VMEM((2, 1, LANES), f32),
+            pltpu.VMEM((1, LANES), f32),
             pltpu.VMEM((1, LANES), f32),
             pltpu.VMEM((1, LANES), f32),
             pltpu.VMEM((3 * down, LANES), f32),
-            dma((6,)), dma, dma, dma, dma,
+            pltpu.VMEM((3 * down, LANES), f32),
+            pltpu.VMEM((2 * down, LANES), f32),
+            pltpu.VMEM((1, LANES), f32),
+            pltpu.VMEM((5, 1, LANES), f32),
+            dma((8,)), dma, dma, dma, dma,
             pltpu.SemaphoreType.REGULAR,
             pltpu.SemaphoreType.REGULAR,
             pltpu.SemaphoreType.REGULAR,

time: 11.3 us -> 11.4 us (level)
  the two profiles are of different devices: /device:TPU:12 before, /device:TPU:9 now
where the time goes in v4:
time: 11.4 us; the launch traced here: 11.2 us
  Pallas kernels  9.88 us (87%)
  between operations  1.3 us (11%)
    pallas_call x1, Pallas kernels, on_device(): call(wrapped[f:f + 1], col_steps[f:f + 1], row_steps[f:f + 1])  7.7 us
    pallas_call x1, Pallas kernels, on_device(): place(*call(wrapped[f:f + 1], col_steps[f:f + 1], row_steps[f:f + 1]))  2.19 us

profile of v4, /device:TPU:9, one launch (start us, length us, event | category | flops | bytes accessed | tf_op | source)
XLA Modules:
  0.0 11.2 jit_solution(3869589562915997588)
XLA Ops:
  1.3 7.7 %shard_map.37 = (f32[1024,1024]{1,0:T(8,128)S(1)}, f32[8,128]{1,0:T(8,128)S(1)}) custom-call(f32[1,1024,1024]{2,1,0:T(8,128)} %refs_0_.1, s32[1,1,1]{2,1,0:T(1,128)S(6)} %copy.4.refs_1_, s32[1,1,1]{2,1,0:T(1,128)S(6)} %copy.5.refs_2_), custom_call_target="tpu_custom_call" | custom-call | tf_op jit(solution)/shard_map/pallas_call | solution.py:835
  9.0 2.2 %shard_map.38 = f32[1024,1024]{1,0:T(8,128)} custom-call(f32[1024,1024]{1,0:T(8,128)S(1)} %get-tuple-element.7.integ, f32[8,128]{1,0:T(8,128)S(1)} %get-tuple-element.8.offset), custom_call_target="tpu_custom_call" | custom-call | tf_op jit(solution)/shard_map/pallas_call | solution.py:835

commit v5 on v4

--- a/solution.py
+++ b/solution.py
@@ -81,7 +81,7 @@
     cells, left_out, right_in, corner_above, corner_left, tops, bottom_out, bottoms, inner_row,
     floors, row_sums, steps_across, steps_down, mine_h, mine_y, row_h, top_h, col_h, left_d, carried, ends, ends_in, pair_in, first_inner, left_sums,
     link_recv, top_recv, bottom_recv, row_recv, far_recv, row_in, col_in, far_in,
-    load_sem, link_send, top_send, bottom_send, h_send, c_send, d_send,
+    load_sem, link_send, top_send, bottom_send, h_send, c_send, d_send, back_send,
 ):
     row_name, col_name = names
     grid_rows, grid_cols = sizes
@@ -288,25 +288,25 @@
         return send(bottom_out, bottoms.at[my_row], bottom_send.at[r], bottom_recv, (r, c))
 
     def row_copy(r, c):
-        return send(mine_h.at[1], row_h.at[my_col], h_send.at[r * grid_cols + c], row_recv, (r, c))
+        return send(mine_h.at[1], row_h.at[my_col], h_send.at[r], row_recv, (r, c))
 
     def far_copy(r, c):
-        return send(mine_h.at[1], top_h.at[my_col], h_send.at[r * grid_cols + c], far_recv, (r, c))
+        return send(mine_h.at[1], top_h.at[my_col], h_send.at[r], far_recv, (r, c))
 
     def origin_copy(r, c):
-        return send(mine_h.at[1], row_h.at[0], h_send.at[r * grid_cols + c], link_recv.at[5], (r, c))
+        return send(mine_h.at[1], row_h.at[0], h_send.at[r], link_recv.at[5], (r, c))
 
     def relay_in(r, c):
         return send(mine_h.at[2], col_h, c_send.at[r], link_recv.at[6], (r, c))
 
     def relay_left(r, c):
-        return send(mine_h.at[0], col_h, h_send.at[r * grid_cols + c], link_recv.at[6], (r, c))
+        return send(mine_h.at[0], col_h, h_send.at[r], link_recv.at[6], (r, c))
 
     def relay_back(r, c):
-        return send(mine_h.at[0], row_h.at[1], h_send.at[r * grid_cols + c], link_recv.at[5], (r, c))
+        return send(mine_h.at[0], row_h.at[1], back_send, link_recv.at[5], (r, c))
 
     def left_copy(r, c):
-        return send(mine_y, left_d, d_send.at[c], link_recv.at[7], (r, c))
+        return send(mine_y, left_d, d_send, link_recv.at[7], (r, c))
 
     def push_tops(low, high, act):
         along_col(jnp.where(has_above, low, grid_rows), high, act)
@@ -685,16 +685,25 @@
         push_tops(my_row + 1, grid_rows, lambda r, c: top_copy(r, c).wait_send())
         along_col(my_row + 1, grid_rows, lambda r, c: bottom_copy(r, c).wait_send())
         along_col(to_relay, grid_rows, lambda r, c: relay_in(r, c).wait_send())
-        along_row(to_row, row_end, lambda r, c: row_copy(r, c).wait_send())
-        pair_places(lambda r, c: origin_copy(r, c).wait_send())
-        left_below(lambda r, c: relay_left(r, c).wait_send())
+
+        def sent(semaphore, count):
+            for n in range(1, grid_cols):
+
+                @pl.when(count == n)
+                def _():
+                    line = row_h.at[pl.ds(0, n)]
+                    pltpu.make_async_copy(line, line, semaphore).wait()
+
+        told = jnp.where(origin, 2, jnp.maximum(row_end - to_row, 0))
+        sent(h_send.at[my_row], told)
+        sent(d_send, jnp.maximum(grid_cols - to_right, 0))
+        far_told = grid_cols - 1 - my_col + jnp.where(second, 1, 0)
+        far_low = jnp.where(direct_top, 1, grid_rows)
+        span(far_low, grid_rows, lambda r: sent(h_send.at[r], far_told))
 
         @pl.when(second)
         def _():
             relay_back(0, 2).wait_send()
-
-        far_below(lambda r, c: far_copy(r, c).wait_send())
-        along_row(to_right, grid_cols, lambda r, c: left_copy(r, c).wait_send())
 
     with jax.named_scope("hear"):
         hear(row_h, row_recv, 3, jnp.where(has_above, 0, my_col - 3))
@@ -738,8 +747,14 @@
         offset[...] = jnp.broadcast_to(here, offset.shape)
 
 
-def place_kernel(integ, offset, out, ready, sems):
-    parts = sems.shape[0]
+def place_kernel(parts, integ, offset, out, ready):
+    pl.run_scoped(
+        functools.partial(place_rows, parts, integ, offset, out, ready),
+        pltpu.SemaphoreType.DMA((parts,)),
+    )
+
+
+def place_rows(parts, integ, offset, out, ready, sems):
     step = integ.shape[0] // parts
     shift = offset[0:1, 0:1]
     copies = []
@@ -765,8 +780,10 @@
     def with_local_semaphores(*refs):
         pl.run_scoped(
             functools.partial(edge_kernel, names, sizes, rows_step, cols_step, *refs),
+            dma((8,)), dma, dma, dma, dma,
+            pltpu.SemaphoreType.REGULAR, pltpu.SemaphoreType.REGULAR, pltpu.SemaphoreType.REGULAR,
             dma((tile_rows // rows_step + 5,)), dma((5,)), dma((grid_rows,)), dma((grid_rows,)),
-            dma((grid_rows * grid_cols,)), dma((grid_rows,)), dma((grid_cols,)),
+            dma((grid_rows,)), dma((grid_rows,)), dma, dma,
         )
 
     call = pl.pallas_call(
@@ -810,10 +827,6 @@
             pltpu.VMEM((2 * down, LANES), f32),
             pltpu.VMEM((1, LANES), f32),
             pltpu.VMEM((5, 1, LANES), f32),
-            dma((8,)), dma, dma, dma, dma,
-            pltpu.SemaphoreType.REGULAR,
-            pltpu.SemaphoreType.REGULAR,
-            pltpu.SemaphoreType.REGULAR,
         ],
         compiler_params=pltpu.CompilerParams(
             collective_id=0, has_side_effects=True, vmem_limit_bytes=57 * 1024 * 1024
@@ -821,14 +834,11 @@
     )
     parts = math.gcd(tile_rows // 8, 16)
     place = pl.pallas_call(
-        place_kernel,
+        functools.partial(place_kernel, parts),
         out_shape=jax.ShapeDtypeStruct((tile_rows, tile_cols), f32),
         in_specs=[pl.BlockSpec(memory_space=pltpu.VMEM), pl.BlockSpec(memory_space=pltpu.VMEM)],
         out_specs=pl.BlockSpec(memory_space=pltpu.HBM),
-        scratch_shapes=[
-            pltpu.VMEM((tile_rows, tile_cols), f32),
-            pltpu.SemaphoreType.DMA((parts,)),
-        ],
+        scratch_shapes=[pltpu.VMEM((tile_rows, tile_cols), f32)],
         compiler_params=pltpu.CompilerParams(vmem_limit_bytes=24 * 1024 * 1024),
     )
     outs = [

time: 11.4 us -> 11 us (0.965)
  the two profiles are of different devices: /device:TPU:9 before, /device:TPU:12 now
where the time goes in v5:
time: 11 us; the launch traced here: 10.8 us
  Pallas kernels  9.48 us (86%)
  between operations  1.3 us (12%)
    pallas_call x1, Pallas kernels, on_device(): call(wrapped[f:f + 1], col_steps[f:f + 1], row_steps[f:f + 1])  7.44 us
    pallas_call x1, Pallas kernels, on_device(): place(*call(wrapped[f:f + 1], col_steps[f:f + 1], row_steps[f:f + 1]))  2.05 us

profile of v5, /device:TPU:12, one launch (start us, length us, event | category | flops | bytes accessed | tf_op | source)
XLA Modules:
  0.0 10.8 jit_solution(17410835101002669819)
XLA Ops:
  1.3 7.4 %shard_map.37 = (f32[1024,1024]{1,0:T(8,128)S(1)}, f32[8,128]{1,0:T(8,128)S(1)}) custom-call(f32[1,1024,1024]{2,1,0:T(8,128)} %refs_0_.1, s32[1,1,1]{2,1,0:T(1,128)S(6)} %copy.4.refs_1_, s32[1,1,1]{2,1,0:T(1,128)S(6)} %copy.5.refs_2_), custom_call_target="tpu_custom_call" | custom-call | tf_op jit(solution)/shard_map/pallas_call | solution.py:845
  8.7 2.0 %shard_map.38 = f32[1024,1024]{1,0:T(8,128)} custom-call(f32[1024,1024]{1,0:T(8,128)S(1)} %get-tuple-element.7.integ, f32[8,128]{1,0:T(8,128)S(1)} %get-tuple-element.8.offset), custom_call_target="tpu_custom_call" | custom-call | tf_op jit(solution)/shard_map/pallas_call | solution.py:845

commit v6 on v5

--- a/solution.py
+++ b/solution.py
@@ -221,6 +221,7 @@
     last = (my_row == 0) & (my_col < 2) & jnp.logical_not(first)
     between = jnp.logical_not(first | last)
 
+    feeds = paired | before_second
     weighs_late = last | before_second
 
     def enter():
@@ -413,6 +414,14 @@
         down_weights()
         push_bottoms()
 
+    def push_further_bottoms():
+        along_col(near, grid_rows, lambda r, c: bottom_copy(r, c).start())
+
+    def weigh_after():
+        with jax.named_scope("weigh_after"):
+            pl.when(has_below)(weigh_bottom)
+            push_further_bottoms()
+
     def push_further_tops():
         await_signals(col_in, grid_rows - near)
         pl.when(tail)(lambda: push(1))
@@ -428,7 +437,7 @@
             loads[q + 3].wait()
         with jax.named_scope(f"floors_{q}"):
             lax.fori_loop(
-                q * per_chunk, (q + 1) * per_chunk, strip, 0, unroll=math.gcd(per_chunk, 8)
+                q * per_chunk, (q + 1) * per_chunk, strip, 0, unroll=math.gcd(per_chunk, 16)
             )
         if q == (chunks - 1) // 2:
             with jax.named_scope("enter_2"):
@@ -440,11 +449,11 @@
                     push_down()
 
     with jax.named_scope("corner_left"):
-        pl.when(has_left & has_below & weighs_late)(weigh_bottom)
+        pl.when(has_left & has_below & weighs_late & jnp.logical_not(feeds))(weigh_bottom)
 
     with jax.named_scope("col_in"):
         pl.when(jnp.logical_not(tail))(push_further_tops)
-        along_col(near, grid_rows, lambda r, c: bottom_copy(r, c).start())
+        pl.when(jnp.logical_not(feeds))(push_further_bottoms)
 
     relays = (my_col > 0) & (my_col < 4)
     to_relay = jnp.where(paired | second, 1, grid_rows)
@@ -502,6 +511,8 @@
             ends[2 * down :, :] = end_count
             first_inner[...] = inner_col[0:1, :]
             push(3)
+
+        pl.when(paired)(weigh_after)
 
     def across_mean():
         with jax.named_scope("halo_0"):
@@ -550,6 +561,8 @@
         with jax.named_scope("row_in"):
             await_row()
             along_row(to_row, row_end, lambda r, c: row_copy(r, c).start())
+
+        pl.when(before_second)(weigh_after)
 
     def tell_far():
         with jax.named_scope("far_in"):

time: 11 us -> 11 us (level)
  the two profiles are of different devices: /device:TPU:12 before, /device:TPU:10 now
where the time goes in v6:
time: 11 us; the launch traced here: 10.8 us
  Pallas kernels  9.52 us (87%)
  between operations  1.3 us (12%)
    pallas_call x1, Pallas kernels, on_device(): call(wrapped[f:f + 1], col_steps[f:f + 1], row_steps[f:f + 1])  7.47 us
    pallas_call x1, Pallas kernels, on_device(): place(*call(wrapped[f:f + 1], col_steps[f:f + 1], row_steps[f:f + 1]))  2.05 us

profile of v6, /device:TPU:10, one launch (start us, length us, event | category | flops | bytes accessed | tf_op | source)
XLA Modules:
  0.0 10.8 jit_solution(8829799217734201313)
XLA Ops:
  1.3 7.5 %shard_map.37 = (f32[1024,1024]{1,0:T(8,128)S(1)}, f32[8,128]{1,0:T(8,128)S(1)}) custom-call(f32[1,1024,1024]{2,1,0:T(8,128)} %refs_0_.1, s32[1,1,1]{2,1,0:T(1,128)S(6)} %copy.4.refs_1_, s32[1,1,1]{2,1,0:T(1,128)S(6)} %copy.5.refs_2_), custom_call_target="tpu_custom_call" | custom-call | tf_op jit(solution)/shard_map/pallas_call | solution.py:858
  8.8 2.0 %shard_map.38 = f32[1024,1024]{1,0:T(8,128)} custom-call(f32[1024,1024]{1,0:T(8,128)S(1)} %get-tuple-element.7.integ, f32[8,128]{1,0:T(8,128)S(1)} %get-tuple-element.8.offset), custom_call_target="tpu_custom_call" | custom-call | tf_op jit(solution)/shard_map/pallas_call | solution.py:858

commit v7 on v6

--- a/solution.py
+++ b/solution.py
@@ -80,7 +80,7 @@
     integ, offset,
     cells, left_out, right_in, corner_above, corner_left, tops, bottom_out, bottoms, inner_row,
     floors, row_sums, steps_across, steps_down, mine_h, mine_y, row_h, top_h, col_h, left_d, carried, ends, ends_in, pair_in, first_inner, left_sums,
-    link_recv, top_recv, bottom_recv, row_recv, far_recv, row_in, col_in, far_in,
+    link_recv, top_recv, bottom_recv, row_recv, far_recv, row_in, tail_in, col_in, far_in,
     load_sem, link_send, top_send, bottom_send, h_send, c_send, d_send, back_send,
 ):
     row_name, col_name = names
@@ -239,7 +239,11 @@
             push(0)
             push(4)
 
-        along_row(first_left, jnp.where(greets_left, my_col - 1, my_col), greet(row_in))
+        def greet_row(semaphore):
+            along_row(first_left, jnp.where(greets_left, my_col - 1, my_col), greet(semaphore))
+
+        pl.when(tail_col)(lambda: greet_row(tail_in))
+        pl.when(jnp.logical_not(tail_col))(lambda: greet_row(row_in))
         greet_above(col_in, True)
         direct_tops(greet(far_in))
 
@@ -553,14 +557,30 @@
 
             along_col(to_relay, grid_rows, lambda r, c: relay_in(r, c).start())
 
-    def await_row():
-        known = jnp.where(knows_right, my_col + 1, my_col)
-        await_signals(row_in, jnp.where(lead, 0, grid_cols - 1 - known))
+    inner_cols = grid_cols - 2
+    known = jnp.where(knows_right, my_col + 1, my_col)
+    inner_unknown = jnp.where(lead, 0, jnp.maximum(inner_cols - 1 - known, 0))
+    tail_unknown = jnp.where(lead, 0, grid_cols - 1 - known - inner_unknown)
+
+    def tell_inner():
+        await_signals(row_in, inner_unknown)
+        along_row(to_right, inner_cols, lambda r, c: left_copy(r, c).start())
+        along_row(to_row, jnp.minimum(row_end, inner_cols), lambda r, c: row_copy(r, c).start())
+
+    def tell_tail():
+        with jax.named_scope("tail_tell"):
+            await_signals(tail_in, tail_unknown)
+            along_row(
+                jnp.maximum(to_right, inner_cols), grid_cols, lambda r, c: left_copy(r, c).start()
+            )
+            along_row(
+                jnp.maximum(to_row, inner_cols), row_end, lambda r, c: row_copy(r, c).start()
+            )
 
     def tell():
         with jax.named_scope("row_in"):
-            await_row()
-            along_row(to_row, row_end, lambda r, c: row_copy(r, c).start())
+            tell_inner()
+            tell_tail()
 
         pl.when(before_second)(weigh_after)
 
@@ -620,9 +640,7 @@
         with jax.named_scope("base_left"):
             sum_above()
         with jax.named_scope("row_in_left"):
-            await_row()
-            along_row(to_right, grid_cols, lambda r, c: left_copy(r, c).start())
-            along_row(to_row, row_end, lambda r, c: row_copy(r, c).start())
+            tell_inner()
 
     def integrate(low, high):
         with jax.named_scope(f"integrate_{low}"):
@@ -652,9 +670,9 @@
 
     odd_row = lax.rem(my_row, 2) == 1
     far_early = (my_row == 0) & (my_col > 3)
-    split = (even_row & has_left) | (tail_col & odd_row)
+    split = (even_row & has_left) | (tail_col & odd_row) | (lax.rem(my_col, 2) == 1)
     half = (chunks + 1) // 2
-    never = 10
+    never = 11
     at_left, at_top, at_pair, at_split, at_second, otherwise = range(6)
     kind = jnp.where(second, at_second, jnp.where(split, at_split, otherwise))
     kind = jnp.where(pair, jnp.where(paired, at_top, at_pair), kind)
@@ -668,14 +686,15 @@
 
     order = (
         (left_start, pick(0, never, never, never, never, never)),
-        (left_finish, pick(2, never, never, never, never, never)),
+        (left_finish, pick(jnp.where(my_row == 1, 1, 2), never, never, never, never, never)),
+        (tell_tail, pick(3, never, never, never, never, never)),
         (across, jnp.where(has_right, pick(never, 0, 1, 1, 1, 0), never)),
         (across_mean, jnp.where(has_right, pick(never, never, 2, 2, 2, 1), never)),
         (across_pair, pick(never, 2, never, never, 3, never)),
         (tell, pick(never, never, 3, 3, 4, 2)),
-        (functools.partial(integrate, 0, half), pick(1, 1, 0, 0, 0, jnp.where(far_early, 4, 3))),
+        (functools.partial(integrate, 0, half), pick(jnp.where(my_row == 1, 2, 1), 1, 0, 0, 0, jnp.where(far_early, 4, 3))),
         (tell_far, jnp.where(direct_top, jnp.where(second, 5, jnp.where(far_early, 3, 4)), never)),
-        (functools.partial(integrate, half, chunks), pick(3, 3, 5, 4, 6, 5)),
+        (functools.partial(integrate, half, chunks), pick(4, 3, 5, 4, 6, 5)),
         (down_sum, pick(never, never, 4, 5, never, 6)),
     )
 
@@ -794,7 +813,7 @@
         pl.run_scoped(
             functools.partial(edge_kernel, names, sizes, rows_step, cols_step, *refs),
             dma((8,)), dma, dma, dma, dma,
-            pltpu.SemaphoreType.REGULAR, pltpu.SemaphoreType.REGULAR, pltpu.SemaphoreType.REGULAR,
+            *[pltpu.SemaphoreType.REGULAR] * 4,
             dma((tile_rows // rows_step + 5,)), dma((5,)), dma((grid_rows,)), dma((grid_rows,)),
             dma((grid_rows,)), dma((grid_rows,)), dma, dma,
         )

time: 11 us -> 10.8 us (0.982)
  the two profiles are of different devices: /device:TPU:10 before, /device:TPU:12 now
where the time goes in v7:
time: 10.8 us; the launch traced here: 10.7 us
  Pallas kernels  9.38 us (87%)
  between operations  1.3 us (12%)
    pallas_call x1, Pallas kernels, on_device(): call(wrapped[f:f + 1], col_steps[f:f + 1], row_steps[f:f + 1])  7.33 us
    pallas_call x1, Pallas kernels, on_device(): place(*call(wrapped[f:f + 1], col_steps[f:f + 1], row_steps[f:f + 1]))  2.05 us

profile of v7, /device:TPU:12, one launch (start us, length us, event | category | flops | bytes accessed | tf_op | source)
XLA Modules:
  0.0 10.7 jit_solution(3239541030789134578)
XLA Ops:
  1.3 7.3 %shard_map.37 = (f32[1024,1024]{1,0:T(8,128)S(1)}, f32[8,128]{1,0:T(8,128)S(1)}) custom-call(f32[1,1024,1024]{2,1,0:T(8,128)} %refs_0_.1, s32[1,1,1]{2,1,0:T(1,128)S(6)} %copy.4.refs_1_, s32[1,1,1]{2,1,0:T(1,128)S(6)} %copy.5.refs_2_), custom_call_target="tpu_custom_call" | custom-call | tf_op jit(solution)/shard_map/pallas_call | solution.py:877
  8.6 2.0 %shard_map.38 = f32[1024,1024]{1,0:T(8,128)} custom-call(f32[1024,1024]{1,0:T(8,128)S(1)} %get-tuple-element.7.integ, f32[8,128]{1,0:T(8,128)S(1)} %get-tuple-element.8.offset), custom_call_target="tpu_custom_call" | custom-call | tf_op jit(solution)/shard_map/pallas_call | solution.py:877

commit v8 on v7

--- a/solution.py
+++ b/solution.py
@@ -328,12 +328,13 @@
         )
 
     def push_down():
+
+        @pl.when(has_below & jnp.logical_not(has_left))
+        def _():
+            push_bottoms()
+
         pl.when(jnp.logical_not(tail))(lambda: push(1))
         push(2)
-
-        @pl.when(has_below & jnp.logical_not(has_left))
-        def _():
-            push_bottoms()
 
     def row_line(row):
         return jnp.concatenate(
@@ -864,7 +865,7 @@
             collective_id=0, has_side_effects=True, vmem_limit_bytes=57 * 1024 * 1024
         ),
     )
-    parts = math.gcd(tile_rows // 8, 16)
+    parts = math.gcd(tile_rows // 8, 32)
     place = pl.pallas_call(
         functools.partial(place_kernel, parts),
         out_shape=jax.ShapeDtypeStruct((tile_rows, tile_cols), f32),

time: 10.8 us -> 10.8 us (level)
  no operation moved by 1% of the time
where the time goes in v8:
time: 10.8 us; the launch traced here: 10.7 us
  Pallas kernels  9.36 us (87%)
  between operations  1.3 us (12%)
    pallas_call x1, Pallas kernels, on_device(): call(wrapped[f:f + 1], col_steps[f:f + 1], row_steps[f:f + 1])  7.33 us
    pallas_call x1, Pallas kernels, on_device(): place(*call(wrapped[f:f + 1], col_steps[f:f + 1], row_steps[f:f + 1]))  2.02 us

profile of v8, /device:TPU:12, one launch (start us, length us, event | category | flops | bytes accessed | tf_op | source)
XLA Modules:
  0.0 10.7 jit_solution(2736380153104078373)
XLA Ops:
  1.3 7.3 %shard_map.37 = (f32[1024,1024]{1,0:T(8,128)S(1)}, f32[8,128]{1,0:T(8,128)S(1)}) custom-call(f32[1,1024,1024]{2,1,0:T(8,128)} %refs_0_.1, s32[1,1,1]{2,1,0:T(1,128)S(6)} %copy.4.refs_1_, s32[1,1,1]{2,1,0:T(1,128)S(6)} %copy.5.refs_2_), custom_call_target="tpu_custom_call" | custom-call | tf_op jit(solution)/shard_map/pallas_call | solution.py:878
  8.6 2.0 %shard_map.38 = f32[1024,1024]{1,0:T(8,128)} custom-call(f32[1024,1024]{1,0:T(8,128)S(1)} %get-tuple-element.7.integ, f32[8,128]{1,0:T(8,128)S(1)} %get-tuple-element.8.offset), custom_call_target="tpu_custom_call" | custom-call | tf_op jit(solution)/shard_map/pallas_call | solution.py:878
